TPU v7x, 128 devices: a whole 4x4x4 slice. The times are simulated.
128 devices in a mesh: dp: 1, row: 16 (over z, y), col: 8 (over x, core).
Axes of the slice: x: 4, y: 4, z: 4, core: 2. Of those that a mesh axis runs over, the one named last changes fastest.
Arguments:
- hidden: bfloat16 [128, 256, 2048], P(('dp', 'row', 'col'))
- positions: int32 [128, 256], P(('dp', 'row', 'col'))
- segments: int32 [128, 256], P(('dp', 'row', 'col'))
- ln_weight: bfloat16 [2, 2048], replicated
- w_qkv: bfloat16 [2, 2048, 6144], P(None, None, ('row', 'col'))
- w_out: bfloat16 [2, 2048, 2048], P(None, ('row', 'col'))
- w_gate: bfloat16 [2, 2048, 8192], P(None, None, ('row', 'col'))
- w_up: bfloat16 [2, 2048, 8192], P(None, None, ('row', 'col'))
- w_down: bfloat16 [2, 8192, 2048], P(None, ('row', 'col'))
Outputs:
- output 1: bfloat16 [128, 256, 2048], P(('dp', 'row', 'col'))
- output 2: bfloat16 [128, 2, 16, 256, 128], P(('dp', 'row', 'col'))
- output 3: bfloat16 [128, 2, 16, 256, 128], P(('dp', 'row', 'col'))
All inputs are finite; a program needn't handle non-finite values.
Results may differ from a plain program's by a relative error of at most 0.0126783.
Values are sent between devices in bfloat16 or wider.
A program may use at most 1 GiB of HBM per device.

v0:
```python
import jax
import jax.numpy as jnp
from jax import lax
from jax.sharding import PartitionSpec as P

HEAD_DIM = 128
NORM_EPS = 1e-5
ROPE_BASE = 8000000.0


def layer_norm(hidden, norm_gain):
    hidden_f = hidden.astype(jnp.float32)
    mean_val = jnp.mean(hidden_f, axis=-1, keepdims=True)
    centred = hidden_f - mean_val
    var_val = jnp.mean(centred * centred, axis=-1, keepdims=True)
    return (centred * lax.rsqrt(var_val + NORM_EPS) * norm_gain.astype(jnp.float32)).astype(jnp.bfloat16)


def rope_tables(positions):
    inv_freq = ROPE_BASE ** (-2.0 * jnp.arange(HEAD_DIM // 2, dtype=jnp.float32) / HEAD_DIM)
    angles = positions.astype(jnp.float32)[..., None, None] * inv_freq
    return jnp.cos(angles), jnp.sin(angles)


def rotary(heads_in, cos_tab, sin_tab):
    pair_view = heads_in.astype(jnp.float32).reshape(heads_in.shape[:-1] + (heads_in.shape[-1] // 2, 2))
    even_part = pair_view[..., 0]
    odd_part = pair_view[..., 1]
    rotated = jnp.stack([even_part * cos_tab - odd_part * sin_tab, odd_part * cos_tab + even_part * sin_tab], axis=-1)
    return rotated.reshape(heads_in.shape).astype(jnp.bfloat16)


def attention(queries, keys_rot, values, segments):
    batch_rows, seq_len, num_heads, head_dim = queries.shape
    kv_heads = keys_rot.shape[2]
    grouped = queries.reshape(batch_rows, seq_len, kv_heads, num_heads // kv_heads, head_dim)
    scores = jnp.einsum("bskgd,btkd->bkgst", grouped, keys_rot, preferred_element_type=jnp.float32) * head_dim ** -0.5
    token_idx = jnp.arange(seq_len)
    causal = token_idx[None, :] <= token_idx[:, None]
    same_seg = segments[:, None, None, :, None] == segments[:, None, None, None, :]
    scores = jnp.where(causal & same_seg, scores, -1e30)
    attn_probs = jax.nn.softmax(scores, axis=-1).astype(jnp.bfloat16)
    attn_out = jnp.einsum("bkgst,btkd->bskgd", attn_probs, values, preferred_element_type=jnp.float32)
    return attn_out.astype(jnp.bfloat16).reshape(batch_rows, seq_len, num_heads * head_dim)


def project_attend(projected, cos_tab, sin_tab, segments, q_cols, kv_cols):
    batch_rows, seq_len = projected.shape[:2]
    queries = rotary(projected[..., :q_cols].reshape(batch_rows, seq_len, q_cols // HEAD_DIM, HEAD_DIM), cos_tab, sin_tab)
    keys_rot = rotary(projected[..., q_cols:q_cols + kv_cols].reshape(batch_rows, seq_len, kv_cols // HEAD_DIM, HEAD_DIM), cos_tab, sin_tab)
    values = projected[..., q_cols + kv_cols:].reshape(batch_rows, seq_len, kv_cols // HEAD_DIM, HEAD_DIM)
    attn_out = attention(queries, keys_rot, values, segments)
    return attn_out, keys_rot.transpose(0, 2, 1, 3), values.transpose(0, 2, 1, 3)


def solution(mesh):
    group_axes = ("row", "col")
    group_size = mesh.shape["row"] * mesh.shape["col"]
    tok_spec = P(("dp", "row", "col"))
    col_spec = P(None, None, group_axes)
    row_spec = P(None, group_axes, None)

    def device_fn(hidden, positions, segments, ln_weight, w_qkv, w_out, w_gate, w_up, w_down):
        q_cols = w_out.shape[1] * group_size
        num_heads = q_cols // HEAD_DIM
        kv_cols = (w_qkv.shape[2] * group_size // HEAD_DIM - num_heads) // 2 * HEAD_DIM
        cos_tab, sin_tab = rope_tables(positions)
        key_list = []
        value_list = []
        for layer_idx in range(w_qkv.shape[0]):
            normed = layer_norm(hidden, ln_weight[layer_idx])
            full_qkv = lax.all_gather(w_qkv[layer_idx], group_axes, axis=1, tiled=True)
            projected = jnp.einsum("btd,dc->btc", normed, full_qkv, preferred_element_type=jnp.float32).astype(jnp.bfloat16)
            attn_out, key_part, value_part = project_attend(projected, cos_tab, sin_tab, segments, q_cols, kv_cols)
            full_gate = lax.all_gather(w_gate[layer_idx], group_axes, axis=1, tiled=True)
            gate_pre = jnp.einsum("btd,df->btf", normed, full_gate, preferred_element_type=jnp.float32)
            full_up = lax.all_gather(w_up[layer_idx], group_axes, axis=1, tiled=True)
            up_proj = jnp.einsum("btd,df->btf", normed, full_up, preferred_element_type=jnp.float32)
            activated = (jax.nn.silu(gate_pre) * up_proj).astype(jnp.bfloat16)
            full_out = lax.all_gather(w_out[layer_idx], group_axes, axis=0, tiled=True)
            attn_proj = jnp.einsum("btc,cd->btd", attn_out, full_out, preferred_element_type=jnp.float32)
            full_down = lax.all_gather(w_down[layer_idx], group_axes, axis=0, tiled=True)
            mlp_proj = jnp.einsum("btf,fd->btd", activated, full_down, preferred_element_type=jnp.float32)
            hidden = (hidden.astype(jnp.float32) + attn_proj + mlp_proj).astype(jnp.bfloat16)
            key_list.append(key_part)
            value_list.append(value_part)
        return hidden, jnp.stack(key_list, axis=1), jnp.stack(value_list, axis=1)

    return jax.shard_map(device_fn, mesh=mesh, in_specs=(tok_spec, tok_spec, tok_spec, P(), col_spec, row_spec, col_spec, col_spec, row_spec), out_specs=(tok_spec, tok_spec, tok_spec), check_vma=False)
```

profile of v0, /device:TPU:1, one launch (start us, length us, event | category | flops | bytes accessed | tf_op | source)
XLA Modules:
  0.0 1011.5 jit_solution(12098624702901568854)
XLA Ops:
  20.3 87.8 %all-gather.21.cloned.1.call-done = bf16[1,2048,6144]{1,2,0:T(8,128)(2,1)} async-done(((bf16[1,2048,48]{1,2,0:T(8,128)(2,1)}), bf16[1,2048,6144]{1,2,0:T(8,128)(2,1)}) %all-gather.21.cloned.1.call-update) | async-done | bytes 25165840 | tf_op jit(solution)/shard_map/all_gather | solution.py:72
  108.1 12.9 %fusion.41 = bf16[1,256,6144]{2,1,0:T(8,128)(2,1)} fusion(bf16[1,2048,6144]{1,2,0:T(8,128)(2,1)} %all-gather.21.cloned.1.call-done, bf16[1,256,2048]{2,1,0:T(8,128)(2,1)S(1)} %copy-done, f32[2048]{0:T(1024)S(1)} %bitcast.229, f32[256]{0:T(256)S(1)} %add_rsqrt_fusion.1, f32[256]{0:T(256)S(1)} %broadcast_multiply_fusion.1), kind=kOutput, calls=%fused_computation.27 | convolution fusion | flops 6446645248 | bytes 29370368 | tf_op jit(solution)/shard_map/btd,dc->btc/dot_general | solution.py:73
  121.0 4.6 slice_bitcast_fusion.1
  125.5 6.0 copy.24
  140.0 6.0 copy.26
  162.8 54.0 %all-gather.25.cloned.1.call-done = bf16[1,2048,8192]{1,2,0:T(8,128)(2,1)} async-done(((bf16[1,2048,64]{1,2,0:T(8,128)(2,1)}), bf16[1,2048,8192]{1,2,0:T(8,128)(2,1)}) %all-gather.25.cloned.1.call-update) | async-done | bytes 33554448 | tf_op jit(solution)/shard_map/all_gather | solution.py:75
  216.8 17.5 %fusion.10 = f32[256,8192]{1,0:T(8,128)} fusion(bf16[1,2048,8192]{1,2,0:T(8,128)(2,1)} %all-gather.25.cloned.1.call-done, bf16[1,256,2048]{2,1,0:T(8,128)(2,1)S(1)} %copy-done, f32[2048]{0:T(1024)S(1)} %bitcast.230, f32[256]{0:T(256)S(1)} %add_rsqrt_fusion.1, f32[256]{0:T(256)S(1)} %broadcast_multiply_fusion.1), kind=kOutput, calls=%fused_computation.10 | convolution fusion | flops 8592556032 | bytes 43001856 | tf_op jit(solution)/shard_map/btd,df->btf/dot_general | solution.py:76
  234.3 91.1 %all-gather.27.cloned.1.call-done = bf16[1,2048,8192]{1,2,0:T(8,128)(2,1)} async-done(((bf16[1,2048,64]{1,2,0:T(8,128)(2,1)}), bf16[1,2048,8192]{1,2,0:T(8,128)(2,1)}) %all-gather.27.cloned.1.call-update) | async-done | bytes 33554448 | tf_op jit(solution)/shard_map/all_gather | solution.py:77
  325.5 108.5 %all-gather.29.cloned.1.call-done = bf16[1,8192,2048]{2,1,0:T(8,128)(2,1)} async-done(((bf16[1,64,2048]{2,1,0:T(8,128)(2,1)}), bf16[1,8192,2048]{2,1,0:T(8,128)(2,1)}) %all-gather.29.cloned.1.call-update) | async-done | bytes 33554448 | tf_op jit(solution)/shard_map/all_gather | solution.py:82
  434.0 29.3 %fusion.54 = f32[1,256,2048]{2,1,0:T(8,128)} fusion(bf16[1,8192,2048]{2,1,0:T(8,128)(2,1)} %all-gather.29.cloned.1.call-done, bf16[1,2048,8192]{1,2,0:T(8,128)(2,1)} %all-gather.27.cloned.1.call-done, f32[256,8192]{1,0:T(8,128)} %fusion.10, bf16[1,256,2048]{2,1,0:T(8,128)(2,1)S(1)} %copy-done, f32[2048]{0:T(1024)S(1)} %bitcast.231, ...), kind=kOutput, calls=%fused_computation.46 | convolution fusion | flops 17195073536 | bytes 78653440 | tf_op jit(solution)/shard_map/btf,fd->btd/dot_general | solution.py:83
  463.3 42.4 %all-gather.23.cloned.1.call-done = bf16[1,2048,2048]{2,1,0:T(8,128)(2,1)} async-done(((bf16[1,16,2048]{2,1,0:T(8,128)(2,1)}), bf16[1,2048,2048]{2,1,0:T(8,128)(2,1)}) %all-gather.23.cloned.1.call-update) | async-done | bytes 8388624 | tf_op jit(solution)/shard_map/all_gather | solution.py:80
  505.7 6.5 convert_reduce_fusion
  512.6 86.4 %all-gather.31.cloned.1.call-done = bf16[1,2048,6144]{1,2,0:T(8,128)(2,1)} async-done(((bf16[1,2048,48]{1,2,0:T(8,128)(2,1)}), bf16[1,2048,6144]{1,2,0:T(8,128)(2,1)}) %all-gather.31.cloned.1.call-update) | async-done | bytes 25165840 | tf_op jit(solution)/shard_map/all_gather | solution.py:72
  599.1 12.9 %fusion.38 = bf16[1,256,6144]{2,1,0:T(8,128)(2,1)} fusion(bf16[1,2048,6144]{1,2,0:T(8,128)(2,1)} %all-gather.31.cloned.1.call-done, bf16[1,256,2048]{2,1,0:T(8,128)(2,1)S(1)} %get-tuple-element.39, f32[2048]{0:T(1024)S(1)} %bitcast.226, f32[256]{0:T(256)S(1)} %add_rsqrt_fusion, f32[256]{0:T(256)S(1)} %broadcast_multiply_fusion), kind=kOutput, calls=%fused_computation.26 | convolution fusion | flops 6446645248 | bytes 29370368 | tf_op jit(solution)/shard_map/btd,dc->btc/dot_general | solution.py:73
  612.0 5.2 slice_bitcast_fusion
  617.2 4.7 copy.32
  632.5 4.7 copy.34
  652.9 54.9 %all-gather.35.cloned.1.call-done = bf16[1,2048,8192]{1,2,0:T(8,128)(2,1)} async-done(((bf16[1,2048,64]{1,2,0:T(8,128)(2,1)}), bf16[1,2048,8192]{1,2,0:T(8,128)(2,1)}) %all-gather.35.cloned.1.call-update) | async-done | bytes 33554448 | tf_op jit(solution)/shard_map/all_gather | solution.py:75
  707.8 17.5 %fusion.4 = f32[256,8192]{1,0:T(8,128)} fusion(bf16[1,2048,8192]{1,2,0:T(8,128)(2,1)} %all-gather.35.cloned.1.call-done, bf16[1,256,2048]{2,1,0:T(8,128)(2,1)S(1)} %get-tuple-element.39, f32[2048]{0:T(1024)S(1)} %bitcast.227, f32[256]{0:T(256)S(1)} %add_rsqrt_fusion, f32[256]{0:T(256)S(1)} %broadcast_multiply_fusion), kind=kOutput, calls=%fused_computation.4 | convolution fusion | flops 8592556032 | bytes 43001856 | tf_op jit(solution)/shard_map/btd,df->btf/dot_general | solution.py:76
  725.4 91.1 %all-gather.37.cloned.1.call-done = bf16[1,2048,8192]{1,2,0:T(8,128)(2,1)} async-done(((bf16[1,2048,64]{1,2,0:T(8,128)(2,1)}), bf16[1,2048,8192]{1,2,0:T(8,128)(2,1)}) %all-gather.37.cloned.1.call-update) | async-done | bytes 33554448 | tf_op jit(solution)/shard_map/all_gather | solution.py:77
  816.5 108.7 %all-gather.39.cloned.1.call-done = bf16[1,8192,2048]{2,1,0:T(8,128)(2,1)} async-done(((bf16[1,64,2048]{2,1,0:T(8,128)(2,1)}), bf16[1,8192,2048]{2,1,0:T(8,128)(2,1)}) %all-gather.39.cloned.1.call-update) | async-done | bytes 33554448 | tf_op jit(solution)/shard_map/all_gather | solution.py:82
  925.1 29.2 %fusion.59 = f32[1,256,2048]{2,1,0:T(8,128)} fusion(bf16[1,8192,2048]{2,1,0:T(8,128)(2,1)} %all-gather.39.cloned.1.call-done, bf16[1,2048,8192]{1,2,0:T(8,128)(2,1)} %all-gather.37.cloned.1.call-done, f32[256,8192]{1,0:T(8,128)} %fusion.4, bf16[1,256,2048]{2,1,0:T(8,128)(2,1)S(1)} %get-tuple-element.39, f32[2048]{0:T(1024)S(1)} %bitcast.228, ...), kind=kOutput, calls=%fused_computation.47 | convolution fusion | flops 17195073536 | bytes 78653440 | tf_op jit(solution)/shard_map/btf,fd->btd/dot_general | solution.py:83
  954.3 42.5 %all-gather.33.cloned.1.call-done = bf16[1,2048,2048]{2,1,0:T(8,128)(2,1)} async-done(((bf16[1,16,2048]{2,1,0:T(8,128)(2,1)}), bf16[1,2048,2048]{2,1,0:T(8,128)(2,1)}) %all-gather.33.cloned.1.call-update) | async-done | bytes 8388624 | tf_op jit(solution)/shard_map/all_gather | solution.py:80
  996.9 7.3 fusion.80
  (88 shorter events, 64.6 us)
Async XLA Ops:
  7.2 7.9 copy-start.9
  7.2 12.0 %copy-start = (bf16[1,256,2048]{2,1,0:T(8,128)(2,1)S(1)}, bf16[1,256,2048]{2,1,0:T(8,128)(2,1)}, u32[]{:S(2)}) copy-start(bf16[1,256,2048]{2,1,0:T(8,128)(2,1)} %param.9) | copy-start | bytes 3145732
  7.2 12.7 %copy-start.10 = (bf16[2,2048]{1,0:T(2,128)(2,1)S(1)}, bf16[2,2048]{1,0:T(2,128)(2,1)}, u32[]{:S(2)}) copy-start(bf16[2,2048]{1,0:T(2,128)(2,1)} %param.12) | copy-start | bytes 24580
  7.2 12.7 %copy-start.12 = (s32[1,256]{1,0:T(1,128)S(1)}, s32[1,256]{1,0:T(1,128)}, u32[]{:S(2)}) copy-start(s32[1,256]{1,0:T(1,128)} %param.10) | copy-start | bytes 3076
  7.2 12.7 %copy-start.11 = (s32[1,256]{1,0:T(1,128)S(1)}, s32[1,256]{1,0:T(1,128)}, u32[]{:S(2)}) copy-start(s32[1,256]{1,0:T(1,128)} %param.11) | copy-start | bytes 3076
  7.2 100.9 %all-gather.21.cloned.1.call-start = ((), (), s32[]{:S(2)}) async-start(), calls=%async_computation | async-start | bytes 25362432 | tf_op jit(solution)/shard_map/all_gather | solution.py:72
  9.2 207.6 %all-gather.25.cloned.1.call-start = ((), (), s32[]{:S(2)}) async-start(), calls=%async_computation.2 | async-start | bytes 33816576 | tf_op jit(solution)/shard_map/all_gather | solution.py:75
  11.1 314.4 %all-gather.27.cloned.1.call-start = ((), (), s32[]{:S(2)}) async-start(), calls=%async_computation.3 | async-start | bytes 33816576 | tf_op jit(solution)/shard_map/all_gather | solution.py:77
  13.0 420.9 %all-gather.29.cloned.1.call-start = ((), (), s32[]{:S(2)}) async-start(), calls=%async_computation.4 | async-start | bytes 33816576 | tf_op jit(solution)/shard_map/all_gather | solution.py:82
  15.0 490.7 %all-gather.23.cloned.1.call-start = ((), (), s32[]{:S(2)}) async-start(), calls=%async_computation.1 | async-start | bytes 8454144 | tf_op jit(solution)/shard_map/all_gather | solution.py:80
  15.8 583.3 %all-gather.31.cloned.1.call-start = ((), (), s32[]{:S(2)}) async-start(), calls=%async_computation.5 | async-start | bytes 25362432 | tf_op jit(solution)/shard_map/all_gather | solution.py:72
  16.3 691.5 %all-gather.35.cloned.1.call-start = ((), (), s32[]{:S(2)}) async-start(), calls=%async_computation.7 | async-start | bytes 33816576 | tf_op jit(solution)/shard_map/all_gather | solution.py:75
  17.1 799.4 %all-gather.37.cloned.1.call-start = ((), (), s32[]{:S(2)}) async-start(), calls=%async_computation.8 | async-start | bytes 33816576 | tf_op jit(solution)/shard_map/all_gather | solution.py:77
  17.8 907.3 %all-gather.39.cloned.1.call-start = ((), (), s32[]{:S(2)}) async-start(), calls=%async_computation.9 | async-start | bytes 33816576 | tf_op jit(solution)/shard_map/all_gather | solution.py:82
  18.6 978.3 %all-gather.33.cloned.1.call-start = ((), (), s32[]{:S(2)}) async-start(), calls=%async_computation.6 | async-start | bytes 8454144 | tf_op jit(solution)/shard_map/all_gather | solution.py:80
  157.5 4.0 copy-start.8
  624.4 5.0 copy-start.3
  628.4 1.0 copy-start.4
  639.5 5.0 copy-start.2
  639.5 6.6 copy-start.1
  646.0 3.2 copy-start.5
  646.0 3.2 copy-start.6
  649.2 2.4 copy-start.7
Sparse Core Ops, SparseCore 0:
  11.7 96.3 all-gather.20
  111.1 105.6 all-gather.24
  219.8 105.6 all-gather.26
  328.3 105.6 all-gather.28
  436.8 68.8 all-gather.22
  508.7 90.3 all-gather.30
  602.1 105.6 all-gather.34
  710.8 105.6 all-gather.36
  819.5 105.6 all-gather.38
  928.0 68.8 all-gather.32
where the time goes:
time: 1020 us; the launch traced here: 1010 us
  waiting for transfers between devices  771 us (76%)
  matrix products  140 us (14%)
  local copies, waits for them, and re-layouts  45.3 us (4%)
  other arithmetic  39.7 us (4%)
  between operations  15 us (1%)
    all_gather x2, waiting for transfers between devices, device_fn(): lax.all_gather(w_down[layer_idx], group_axes, axis=0, tiled=True)  217 us
    all_gather x2, waiting for transfers between devices, device_fn(): full_up = lax.all_gather(w_up[layer_idx], group_axes, axis=1, tiled=True)  182 us
    all_gather x2, waiting for transfers between devices, device_fn(): full_qkv = lax.all_gather(w_qkv[layer_idx], group_axes, axis=1, tiled=True)  174 us
    all_gather x2, waiting for transfers between devices, device_fn(): lax.all_gather(w_gate[layer_idx], group_axes, axis=1, tiled=True)  109 us
    all_gather x2, waiting for transfers between devices, device_fn(): full_out = lax.all_gather(w_out[layer_idx], group_axes, axis=0, tiled=True)  85 us
    dot_general x2, matrix products, device_fn(): jnp.einsum('btf,fd->btd', activated, full_down, preferred_element_type=jn...  58.5 us
    dot_general x2, matrix products, device_fn(): jnp.einsum('btd,df->btf', normed, full_gate, preferred_element_type=jnp.f...  35.1 us
    dot_general x2, matrix products, device_fn(): jnp.einsum('btd,dc->btc', normed, full_qkv, preferred_element_type=jnp.fl...  25.8 us
  transfers between devices with their start and end apart: 10, of which 10 were waited for; matrix products, arithmetic and copies ran while one was open for 21% of the time, Pallas kernels for 0%

commit v1 on v0

v1 whole, which is shorter than its diff:
```python
import jax
import jax.numpy as jnp
from jax import lax
from jax.sharding import PartitionSpec as P

HEAD_DIM = 128
NORM_EPS = 1e-5
ROPE_BASE = 8000000.0
UNIT = 16


def layer_norm(hidden, norm_gain):
    hidden_f = hidden.astype(jnp.float32)
    mean_val = jnp.mean(hidden_f, axis=-1, keepdims=True)
    centred = hidden_f - mean_val
    var_val = jnp.mean(centred * centred, axis=-1, keepdims=True)
    return (centred * lax.rsqrt(var_val + NORM_EPS) * norm_gain.astype(jnp.float32)).astype(jnp.bfloat16)


def rotary(heads_in, cos_tab, sin_tab):
    pair_view = heads_in.astype(jnp.float32).reshape(heads_in.shape[:-1] + (heads_in.shape[-1] // 2, 2))
    even_part = pair_view[..., 0]
    odd_part = pair_view[..., 1]
    rotated = jnp.stack([even_part * cos_tab - odd_part * sin_tab, odd_part * cos_tab + even_part * sin_tab], axis=-1)
    return rotated.reshape(heads_in.shape).astype(jnp.bfloat16)


def solution(mesh):
    n_row, n_col = mesh.shape["row"], mesh.shape["col"]
    n_x = n_col // 2
    group = n_row * n_col
    both = ("row", "col")
    tok_spec = P(("dp", "row", "col"))
    col_spec = P(None, None, both)
    row_spec = P(None, both, None)

    def shift(value, dx):
        return lax.ppermute(value, "col", [(2 * ((x + dx) % n_x) + c, 2 * x + c) for x in range(n_x) for c in range(2)])

    def swap(value):
        return lax.ppermute(value, "col", [(i, i ^ 1) for i in range(n_col)])

    def gather_rel(value):
        half = value.shape[-1] // 2
        up = shift(value, 1)
        down = shift(value, 3)
        far = jnp.concatenate([shift(up[..., :half], 1), shift(down[..., half:], 3)], axis=-1)
        mine = jnp.stack([value, up, down, far])
        other = swap(mine)
        return jnp.stack([mine, other], axis=1)

    def device_fn(hidden, positions, segments, ln_weight, w_qkv, w_out, w_gate, w_up, w_down):
        layers, seq = w_qkv.shape[0], hidden.shape[1]
        model = hidden.shape[2]
        my_col = lax.axis_index("col")
        my_x, my_core = my_col // 2, my_col % 2
        v_idx = UNIT * my_col + lax.axis_index("row")
        qkv_t = w_qkv.transpose(0, 2, 1).reshape(layers, 3, UNIT, model)
        got = []
        for i in range(3):
            perm = []
            for d in range(group):
                u = (3 * d + i) % group
                perm.append((d, n_col * (u % UNIT) + u // UNIT))
            got.append(lax.ppermute(qkv_t[:, i], both, perm))
        got = jnp.stack(got)
        units = [lax.dynamic_index_in_dim(got, (v_idx + 2 * t) % 3, 0, keepdims=False) for t in range(3)]
        out_rows = lax.ppermute(w_out, both, [(d, n_col * (d % UNIT) + d // UNIT) for d in range(group)])
        shard = jnp.concatenate(units + [w_gate.transpose(0, 2, 1), w_up.transpose(0, 2, 1), out_rows, w_down], axis=1)
        full = [lax.all_gather(shard[l], "row", axis=0) for l in range(layers)]

        ids = gather_rel(jnp.stack([positions[0], segments[0]]))
        ids = ids.reshape(n_col, 2, seq)
        inv_freq = ROPE_BASE ** (-2.0 * jnp.arange(HEAD_DIM // 2, dtype=jnp.float32) / HEAD_DIM)
        angles = ids[:, 0].astype(jnp.float32)[..., None, None] * inv_freq
        cos_tab, sin_tab = jnp.cos(angles), jnp.sin(angles)
        tok = jnp.arange(seq)
        allowed = (tok[None, :] <= tok[:, None])[None] & (ids[:, 1][:, :, None] == ids[:, 1][:, None, :])

        x = hidden[0]
        key_list, value_list = [], []
        for l in range(layers):
            w = full[l]
            w_q = w[:, :48].reshape(n_row, 3, UNIT, model)
            w_g = w[:, 48:112]
            w_u = w[:, 112:176]
            w_o = w[:, 176:192]
            w_d = w[:, 192:256]
            normed = layer_norm(x, ln_weight[l])
            rows = gather_rel(normed).reshape(n_col, seq, model)
            proj = jnp.einsum("bsd,rtud->btsru", rows, w_q, preferred_element_type=jnp.float32).astype(jnp.bfloat16)
            proj = proj.reshape(n_col, 3, seq, 2, HEAD_DIM)
            q = rotary(proj[:, 0], cos_tab, sin_tab)
            k = rotary(proj[:, 1], cos_tab, sin_tab)
            v = proj[:, 2]
            scores = jnp.einsum("bshd,bthd->bhst", q, k, preferred_element_type=jnp.float32) * HEAD_DIM ** -0.5
            scores = jnp.where(allowed[:, None], scores, -1e30)
            probs = jax.nn.softmax(scores, axis=-1).astype(jnp.bfloat16)
            o = jnp.einsum("bhst,bthd->bshd", probs, v, preferred_element_type=jnp.float32).astype(jnp.bfloat16)
            o = o.reshape(n_col, seq, n_row, UNIT)
            kv = jnp.stack([k, v]).transpose(1, 0, 3, 2, 4).reshape(n_x, 2, 2, 2, seq, HEAD_DIM)
            theirs = swap(kv[:, 1])
            kv = kv[:, 0]
            first = jnp.where(my_core == 0, kv, theirs)
            second = jnp.where(my_core == 0, theirs, kv)
            pair = jnp.concatenate([first, second], axis=2)
            kv_rel = jnp.stack([pair[0], shift(pair[2], 1), shift(pair[3], 2), shift(pair[1], 3)])
            kv_abs = lax.dynamic_slice_in_dim(jnp.concatenate([kv_rel, kv_rel]), (n_x - my_x) % n_x, n_x, 0)
            kv_abs = kv_abs.transpose(1, 0, 2, 3, 4).reshape(2, 2 * n_col, seq, HEAD_DIM)
            key_list.append(kv_abs[0])
            value_list.append(kv_abs[1])

            gate = jnp.einsum("bsd,rfd->bsrf", rows, w_g, preferred_element_type=jnp.float32)
            up = jnp.einsum("bsd,rfd->bsrf", rows, w_u, preferred_element_type=jnp.float32)
            act = (jax.nn.silu(gate) * up).astype(jnp.bfloat16)
            act = act.reshape(n_x, 2, seq, n_row, 64)
            o = o.reshape(n_x, 2, seq, n_row, UNIT)

            def partial(i):
                p = jnp.einsum("csrf,rfd->csd", act[i], w_d, preferred_element_type=jnp.float32)
                p = p + jnp.einsum("csru,rud->csd", o[i], w_o, preferred_element_type=jnp.float32)
                return p[0] + swap(p[1])

            half = model // 2
            s_up, s_down, s_far, s_own = partial(1), partial(2), partial(3), None
            plus = shift(s_down[:, :half], 3)
            minus = shift(s_up[:, half:], 1)
            plus = shift(plus + s_far[:, :half], 3)
            minus = shift(minus + s_far[:, half:], 1)
            plus = shift(plus + s_up[:, :half], 3)
            minus = shift(minus + s_down[:, half:], 1)
            s_own = partial(0)
            total = jnp.concatenate([plus, minus], axis=-1) + s_own
            x = (x.astype(jnp.float32) + total).astype(jnp.bfloat16)
        return x[None], jnp.stack(key_list)[None], jnp.stack(value_list)[None]

    return jax.shard_map(device_fn, mesh=mesh, in_specs=(tok_spec, tok_spec, tok_spec, P(), col_spec, row_spec, col_spec, col_spec, row_spec), out_specs=(tok_spec, tok_spec, tok_spec), check_vma=False)
```

time: 1020 us -> 676 us (0.66)
  waiting for transfers between devices: 771 us -> 323 us
  starting transfers between devices: 0.4 us -> 73.3 us
  local copies, waits for them, and re-layouts: 45.3 us -> 72.8 us
  other arithmetic: 39.7 us -> 61.2 us
  matrix products: 140 us -> 123 us
    all_gather x10 -> x2, waiting for transfers between devices: 767 us -> 35.5 us  [device_fn(): full = [lax.all_gather(shard[l], 'row', axis=0) for l in range(layers)]]
    ppermute x0 -> x47, waiting for transfers between devices: none -> 287 us  [the longest x30 275 us: shift(): lax.ppermute(value, 'col', [(2 * ((x + dx) % n_x) + c, 2 * x + c) for x i...]
    ppermute x0 -> x47, starting transfers between devices: none -> 73.2 us  [the longest x30 38.4 us: shift(): lax.ppermute(value, 'col', [(2 * ((x + dx) % n_x) + c, 2 * x + c) for x i...]
    dot_general x12 -> x26, matrix products: 140 us -> 123 us  [the longest x8 32.6 us: partial(): jnp.einsum('csrf,rfd->csd', act[i], w_d, preferred_element_type=jnp.float32)]
    convert_element_type x4, local copies, waits for them, and re-layouts: 21.4 us -> 4.87 us  [rotary(): heads_in.astype(jnp.float32)]
    unnamed x27 -> x106, local copies, waits for them, and re-layouts: 3.94 us -> 19.3 us
    add x0 -> x14, other arithmetic: none -> 15.3 us  [the longest x6 9.65 us: partial(): return p[0] + swap(p[1])]
    another operation x4 -> x19, other arithmetic: 9.21 us -> 23.9 us  [the longest x6 21.2 us: gather_rel(): return jnp.stack([mine, other], axis=1)]
  transfers between devices with their start and end apart: 10 -> 49, of which waited for: 10 -> 30; matrix products, arithmetic and copies ran while one was open for 21% -> 35% of each run, Pallas kernels for 0% -> 0%
where the time goes in v1:
time: 676 us; the launch traced here: 669 us
  waiting for transfers between devices  323 us (48%)
  matrix products  123 us (18%)
  starting transfers between devices  73.3 us (11%)
  local copies, waits for them, and re-layouts  72.8 us (11%)
  other arithmetic  61.2 us (9%)
  between operations  15.8 us (2%)
    ppermute x30, waiting for transfers between devices, shift(): lax.ppermute(value, 'col', [(2 * ((x + dx) % n_x) + c, 2 * x + c) for x i...  275 us
    ppermute x30, starting transfers between devices, shift(): lax.ppermute(value, 'col', [(2 * ((x + dx) % n_x) + c, 2 * x + c) for x i...  38.4 us
    all_gather x2, waiting for transfers between devices, device_fn(): full = [lax.all_gather(shard[l], 'row', axis=0) for l in range(layers)]  35.5 us
    dot_general x8, matrix products, partial(): jnp.einsum('csrf,rfd->csd', act[i], w_d, preferred_element_type=jnp.float32)  32.6 us
    dot_general x2, matrix products, device_fn(): jnp.einsum('bsd,rfd->bsrf', rows, w_u, preferred_element_type=jnp.float32)  30.5 us
    dot_general x2, matrix products, device_fn(): jnp.einsum('bsd,rfd->bsrf', rows, w_g, preferred_element_type=jnp.float32)  26.6 us
    another operation x6, other arithmetic, gather_rel(): return jnp.stack([mine, other], axis=1)  21.2 us
    unnamed x106, local copies, waits for them, and re-layouts  19.3 us
  transfers between devices with their start and end apart: 49, of which 30 were waited for; matrix products, arithmetic and copies ran while one was open for 35% of the time, Pallas kernels for 0%

profile of v1, /device:TPU:1, one launch (start us, length us, event | category | flops | bytes accessed | tf_op | source)
XLA Modules:
  0.0 668.6 jit_solution(7498789764976227136)
XLA Ops:
  43.7 22.0 %collective-permute-done = bf16[256,2048]{1,0:T(8,128)(2,1)S(1)} collective-permute-done((bf16[256,2048]{1,0:T(8,128)(2,1)S(1)}, bf16[256,2048]{1,0:T(8,128)(2,1)S(1)}, u32[]{:S(2)}, u32[]{:S(2)}) %collective-permute-start) | collective-permute-done | bytes 1048608 | tf_op jit(solution)/shard_map/ppermute | solution.py:38
  69.9 9.5 %collective-permute-done.2 = bf16[256,1024]{1,0:T(8,128)(2,1)S(1)} collective-permute-done((bf16[256,1024]{1,0:T(8,128)(2,1)S(1)}, bf16[256,1024]{1,0:T(8,128)(2,1)S(1)}, u32[]{:S(2)}, u32[]{:S(2)}) %collective-permute-start.2) | collective-permute-done | bytes 524320 | tf_op jit(solution)/shard_map/ppermute | solution.py:38
  110.0 8.4 %copy.78 = bf16[4,2,256,2048]{3,2,1,0:T(8,128)(2,1)} copy(bf16[4,2,256,2048]{3,2,0,1:T(8,128)(2,1)} %pad_maximum_fusion) | data formatting | bytes 16777216 | tf_op jit(solution)/shard_map/stack | solution.py:50
  118.4 35.4 %all-gather.3.cloned.1.call-done = bf16[16,256,2048]{2,1,0:T(8,128)(2,1)} async-done(((bf16[1,256,2048]{2,1,0:T(8,128)(2,1)}), bf16[16,256,2048]{2,1,0:T(8,128)(2,1)}) %all-gather.3.cloned.1.call-update) | async-done | bytes 16777232 | tf_op jit(solution)/shard_map/all_gather | solution.py:70
  155.7 9.1 %convert_bitcast_fusion.1 = bf16[8,3,256,16,16]{2,4,0,1,3:T(8,128)(2,1)S(1)} fusion(bf16[16,3,16,2048,1]{3,2,4,1,0:T(8,128)(2,1)S(1)} %bitcast.421, bf16[8,256,2048,1,1]{2,1,0,4,3:T(8,128)(2,1)} %bitcast.437), kind=kOutput, calls=%fused_computation.38 | convolution fusion | flops 6444023808 | bytes 14680064 | tf_op jit(solution)/shard_map/bsd,rtud->btsru/dot_general | solution.py:91
  178.8 13.3 %fusion.5 = f32[8,256,16,64]{1,3,2,0:T(8,128)} fusion(bf16[8,256,2048,1]{2,1,3,0:T(8,128)(2,1)} %bitcast.438, bf16[16,256,2048]{2,1,0:T(8,128)(2,1)S(1)} %bitcast.420), kind=kOutput, calls=%fused_computation.15 | convolution fusion | flops 8589934592 | bytes 20971520 | tf_op jit(solution)/shard_map/bsd,rfd->bsrf/dot_general | solution.py:113
  192.1 15.3 %multiply_convert_fusion.1 = bf16[8,256,16,64]{1,3,2,0:T(8,128)(2,1)} fusion(f32[8,256,16,64]{1,3,2,0:T(8,128)} %fusion.5, bf16[8,256,2048,1]{2,1,3,0:T(8,128)(2,1)} %bitcast.439, bf16[16,256,2048]{2,1,0:T(8,128)(2,1)S(1)} %bitcast.420), kind=kOutput, calls=%fused_computation.5 | convolution fusion | flops 8602517504 | bytes 25165824 | tf_op jit(solution)/shard_map/bsd,rfd->bsrf/dot_general | solution.py:114
  231.7 21.3 %collective-permute-done.15 = f32[256,1024]{1,0:T(8,128)S(1)} collective-permute-done((f32[256,1024]{1,0:T(8,128)S(1)}, f32[256,1024]{1,0:T(8,128)S(1)}, u32[]{:S(2)}, u32[]{:S(2)}) %collective-permute-start.15) | collective-permute-done | bytes 1048608 | tf_op jit(solution)/shard_map/ppermute | solution.py:38
  256.3 21.6 %collective-permute-done.17 = f32[256,1024]{1,0:T(8,128)S(1)} collective-permute-done((f32[256,1024]{1,0:T(8,128)S(1)}, f32[256,1024]{1,0:T(8,128)S(1)}, u32[]{:S(2)}, u32[]{:S(2)}) %collective-permute-start.17) | collective-permute-done | bytes 1048608 | tf_op jit(solution)/shard_map/ppermute | solution.py:38
  282.2 18.8 %collective-permute-done.20 = f32[256,1024]{1,0:T(8,128)S(1)} collective-permute-done((f32[256,1024]{1,0:T(8,128)S(1)}, f32[256,1024]{1,0:T(8,128)S(1)}, u32[]{:S(2)}, u32[]{:S(2)}) %collective-permute-start.20) | collective-permute-done | bytes 1048608 | tf_op jit(solution)/shard_map/ppermute | solution.py:38
  306.3 16.6 %collective-permute-done.21 = f32[256,1024]{1,0:T(8,128)S(1)} collective-permute-done((f32[256,1024]{1,0:T(8,128)S(1)}, f32[256,1024]{1,0:T(8,128)S(1)}, u32[]{:S(2)}, u32[]{:S(2)}) %collective-permute-start.21) | collective-permute-done | bytes 1048608 | tf_op jit(solution)/shard_map/ppermute | solution.py:38
  331.9 12.6 %collective-permute-done.22 = f32[256,1024]{1,0:T(8,128)S(1)} collective-permute-done((f32[256,1024]{1,0:T(8,128)S(1)}, f32[256,1024]{1,0:T(8,128)S(1)}, u32[]{:S(2)}, u32[]{:S(2)}) %collective-permute-start.22) | collective-permute-done | bytes 1048608 | tf_op jit(solution)/shard_map/ppermute | solution.py:38
  349.3 17.8 %collective-permute-done.24 = bf16[256,2048]{1,0:T(8,128)(2,1)S(1)} collective-permute-done((bf16[256,2048]{1,0:T(8,128)(2,1)S(1)}, bf16[256,2048]{1,0:T(8,128)(2,1)S(1)}, u32[]{:S(2)}, u32[]{:S(2)}) %collective-permute-start.24) | collective-permute-done | bytes 1048608 | tf_op jit(solution)/shard_map/ppermute | solution.py:38
  404.7 8.5 %copy.92 = bf16[4,2,256,2048]{3,2,1,0:T(8,128)(2,1)} copy(bf16[4,2,256,2048]{3,2,0,1:T(8,128)(2,1)} %pad_maximum_fusion.1) | data formatting | bytes 16777216 | tf_op jit(solution)/shard_map/stack | solution.py:50
  413.3 9.1 %convert_bitcast_fusion = bf16[8,3,256,16,16]{2,4,0,1,3:T(8,128)(2,1)S(1)} fusion(bf16[16,3,16,2048,1]{3,2,4,1,0:T(8,128)(2,1)S(1)} %bitcast.418, bf16[8,256,2048,1,1]{2,1,0,4,3:T(8,128)(2,1)} %bitcast.434), kind=kOutput, calls=%fused_computation.34 | convolution fusion | flops 6444023808 | bytes 14680064 | tf_op jit(solution)/shard_map/bsd,rtud->btsru/dot_general | solution.py:91
  436.3 13.3 %fusion.3 = f32[8,256,16,64]{1,3,2,0:T(8,128)} fusion(bf16[8,256,2048,1]{2,1,3,0:T(8,128)(2,1)} %bitcast.435, bf16[16,256,2048]{2,1,0:T(8,128)(2,1)S(1)} %bitcast.417), kind=kOutput, calls=%fused_computation.10 | convolution fusion | flops 8589934592 | bytes 20971520 | tf_op jit(solution)/shard_map/bsd,rfd->bsrf/dot_general | solution.py:113
  449.6 15.3 %multiply_convert_fusion = bf16[8,256,16,64]{1,3,2,0:T(8,128)(2,1)} fusion(f32[8,256,16,64]{1,3,2,0:T(8,128)} %fusion.3, bf16[8,256,2048,1]{2,1,3,0:T(8,128)(2,1)} %bitcast.436, bf16[16,256,2048]{2,1,0:T(8,128)(2,1)S(1)} %bitcast.417), kind=kOutput, calls=%fused_computation.4 | convolution fusion | flops 8602517504 | bytes 25165824 | tf_op jit(solution)/shard_map/bsd,rfd->bsrf/dot_general | solution.py:114
  500.1 10.6 %collective-permute-done.40 = bf16[2,4,256,128]{2,3,1,0:T(8,128)(2,1)S(1)} collective-permute-done((bf16[2,4,256,128]{2,3,1,0:T(8,128)(2,1)S(1)}, bf16[2,4,256,128]{2,3,1,0:T(8,128)(2,1)S(1)}, u32[]{:S(2)}, u32[]{:S(2)}) %collective-permute-start.40) | collective-permute-done | bytes 524320 | tf_op jit(solution)/shard_map/ppermute | solution.py:38
  512.6 8.6 %collective-permute-start.42 = (bf16[2,4,256,128]{2,3,1,0:T(8,128)(2,1)S(1)}, bf16[2,4,256,128]{2,3,1,0:T(8,128)(2,1)S(1)}, u32[]{:S(2)}, u32[]{:S(2)}) collective-permute-start(bf16[2,4,256,128]{2,3,1,0:T(8,128)(2,1)S(1)} %get-tuple-element.31), channel_id=1, source_target_pairs={{6,0},{7,1},{0,2},{1,3},{2,4},{3,5},{4,6},{5,7},{14,8},{15,9},{8,1... | collective-permute-start | bytes 1572872 | tf_op jit(solution)/shard_map/ppermute | solution.py:38
  535.2 10.8 %collective-permute-done.42 = bf16[2,4,256,128]{2,3,1,0:T(8,128)(2,1)S(1)} collective-permute-done((bf16[2,4,256,128]{2,3,1,0:T(8,128)(2,1)S(1)}, bf16[2,4,256,128]{2,3,1,0:T(8,128)(2,1)S(1)}, u32[]{:S(2)}, u32[]{:S(2)}) %collective-permute-start.42) | collective-permute-done | bytes 524320 | tf_op jit(solution)/shard_map/ppermute | solution.py:38
  548.0 34.0 %collective-permute-done.32 = f32[256,1024]{1,0:T(8,128)S(1)} collective-permute-done((f32[256,1024]{1,0:T(8,128)S(1)}, f32[256,1024]{1,0:T(8,128)S(1)}, u32[]{:S(2)}, u32[]{:S(2)}) %collective-permute-start.32) | collective-permute-done | bytes 1048608 | tf_op jit(solution)/shard_map/ppermute | solution.py:38
  584.7 22.9 %collective-permute-done.35 = f32[256,1024]{1,0:T(8,128)S(1)} collective-permute-done((f32[256,1024]{1,0:T(8,128)S(1)}, f32[256,1024]{1,0:T(8,128)S(1)}, u32[]{:S(2)}, u32[]{:S(2)}) %collective-permute-start.35) | collective-permute-done | bytes 1048608 | tf_op jit(solution)/shard_map/ppermute | solution.py:38
  620.9 11.3 %collective-permute-done.36 = f32[256,1024]{1,0:T(8,128)} collective-permute-done((f32[256,1024]{1,0:T(8,128)}, f32[256,1024]{1,0:T(8,128)}, u32[]{:S(2)}, u32[]{:S(2)}) %collective-permute-start.36) | collective-permute-done | bytes 1048608 | tf_op jit(solution)/shard_map/ppermute | solution.py:38
  647.1 10.4 %collective-permute-done.37 = f32[256,1024]{1,0:T(8,128)} collective-permute-done((f32[256,1024]{1,0:T(8,128)}, f32[256,1024]{1,0:T(8,128)}, u32[]{:S(2)}, u32[]{:S(2)}) %collective-permute-start.37) | collective-permute-done | bytes 1048608 | tf_op jit(solution)/shard_map/ppermute | solution.py:38
  (326 shorter events, 276.2 us)
Async XLA Ops:
  7.2 146.6 %all-gather.3.cloned.1.call-start = ((), (), s32[]{:S(2)}) async-start(), calls=%async_computation | async-start | bytes 17825792 | tf_op jit(solution)/shard_map/all_gather | solution.py:70
  36.9 358.1 %all-gather.5.cloned.1.call-start = ((), (), s32[]{:S(2)}) async-start(), calls=%async_computation.1 | async-start | bytes 17825792 | tf_op jit(solution)/shard_map/all_gather | solution.py:70
  38.6 27.1 %collective-permute-start = (bf16[256,2048]{1,0:T(8,128)(2,1)S(1)}, bf16[256,2048]{1,0:T(8,128)(2,1)S(1)}, u32[]{:S(2)}, u32[]{:S(2)}) collective-permute-start(bf16[256,2048]{1,0:T(8,128)(2,1)S(1)} %fusion.19), channel_id=1, source_target_pairs={{2,0},{3,1},{4,2},{5,3},{6,4},{7,5},{0,6},{1,7},{10,8},{11,9},{12,... | collective-permute-start | bytes 3145736 | tf_op jit(solution)/shard_map/ppermute | solution.py:38
  43.6 25.7 %collective-permute-start.1 = (bf16[256,2048]{1,0:T(8,128)(2,1)S(1)}, bf16[256,2048]{1,0:T(8,128)(2,1)S(1)}, u32[]{:S(2)}, u32[]{:S(2)}) collective-permute-start(bf16[256,2048]{1,0:T(8,128)(2,1)S(1)} %fusion.19), channel_id=1, source_target_pairs={{6,0},{7,1},{0,2},{1,3},{2,4},{3,5},{4,6},{5,7},{14,8},{15,9},{8,1... | collective-permute-start | bytes 3145736 | tf_op jit(solution)/shard_map/ppermute | solution.py:38
  227.4 25.6 %collective-permute-start.15 = (f32[256,1024]{1,0:T(8,128)S(1)}, f32[256,1024]{1,0:T(8,128)S(1)}, u32[]{:S(2)}, u32[]{:S(2)}) collective-permute-start(f32[256,1024]{1,0:T(8,128)S(1)} %slice.454), channel_id=1, source_target_pairs={{6,0},{7,1},{0,2},{1,3},{2,4},{3,5},{4,6},{5,7},{14,8},{15,9},{8,1... | collective-permute-start | bytes 3145736 | tf_op jit(solution)/shard_map/ppermute | solution.py:38
  228.9 27.1 %collective-permute-start.18 = (f32[256,2048]{1,0:T(8,128)S(1)}, f32[256,2048]{1,0:T(8,128)S(1)}, u32[]{:S(2)}, u32[]{:S(2)}) collective-permute-start(f32[256,2048]{1,0:T(8,128)S(1)} %slice_bitcast_fusion.24), channel_id=1, source_target_pairs={{0,1},{1,0},{2,3},{3,2},{4,5},{5,4},{6,7},{7,6},{8,9},{9,8},{10,11... | collective-permute-start | bytes 6291464 | tf_op jit(solution)/shard_map/ppermute | solution.py:41
  253.2 24.8 %collective-permute-start.17 = (f32[256,1024]{1,0:T(8,128)S(1)}, f32[256,1024]{1,0:T(8,128)S(1)}, u32[]{:S(2)}, u32[]{:S(2)}) collective-permute-start(f32[256,1024]{1,0:T(8,128)S(1)} %slice_add_fusion.7), channel_id=1, source_target_pairs={{6,0},{7,1},{0,2},{1,3},{2,4},{3,5},{4,6},{5,7},{14,8},{15,9},{8,1... | collective-permute-start | bytes 3145736 | tf_op jit(solution)/shard_map/ppermute | solution.py:38
  302.5 23.1 %collective-permute-start.23 = (f32[256,2048]{1,0:T(8,128)S(1)}, f32[256,2048]{1,0:T(8,128)S(1)}, u32[]{:S(2)}, u32[]{:S(2)}) collective-permute-start(f32[256,2048]{1,0:T(8,128)S(1)} %slice_bitcast_fusion.22), channel_id=1, source_target_pairs={{0,1},{1,0},{2,3},{3,2},{4,5},{5,4},{6,7},{7,6},{8,9},{9,8},{10,11... | collective-permute-start | bytes 6291464 | tf_op jit(solution)/shard_map/ppermute | solution.py:41
  306.1 25.8 %collective-permute-start.19 = (f32[256,1024]{1,0:T(8,128)S(1)}, f32[256,1024]{1,0:T(8,128)S(1)}, u32[]{:S(2)}, u32[]{:S(2)}) collective-permute-start(f32[256,1024]{1,0:T(8,128)S(1)} %get-tuple-element.39), channel_id=1, source_target_pairs={{6,0},{7,1},{0,2},{1,3},{2,4},{3,5},{4,6},{5,7},{14,8},{15,9},{8,1... | collective-permute-start | bytes 3145736 | tf_op jit(solution)/shard_map/ppermute | solution.py:38
  394.6 98.0 %collective-permute-start.39 = (bf16[4,2,2,256,128]{3,4,2,0,1:T(8,128)(2,1)}, bf16[4,2,2,256,128]{3,4,2,0,1:T(8,128)(2,1)}, u32[]{:S(2)}, u32[]{:S(2)}) collective-permute-start(bf16[4,2,2,256,128]{3,4,2,0,1:T(8,128)(2,1)} %slice_bitcast_fusion.40), channel_id=1, source_target_pairs={{0,1},{1,0},{2,3},{3,2},{4,5},{5,4},{6,7},{7,6},{8,9},{9,8},{10,11... | collective-permute-start | bytes 3145736 | tf_op jit(solution)/shard_map/ppermute | solution.py:41
  426.5 67.7 %collective-permute-start.43 = (bf16[4,2,2,256,128]{3,4,2,0,1:T(8,128)(2,1)}, bf16[4,2,2,256,128]{3,4,2,0,1:T(8,128)(2,1)}, u32[]{:S(2)}, u32[]{:S(2)}) collective-permute-start(bf16[4,2,2,256,128]{3,4,2,0,1:T(8,128)(2,1)} %slice_bitcast_fusion.38), channel_id=1, source_target_pairs={{0,1},{1,0},{2,3},{3,2},{4,5},{5,4},{6,7},{7,6},{8,9},{9,8},{10,11... | collective-permute-start | bytes 3145736 | tf_op jit(solution)/shard_map/ppermute | solution.py:41
  470.2 75.8 %collective-permute-start.33 = (f32[256,2048]{1,0:T(8,128)}, f32[256,2048]{1,0:T(8,128)}, u32[]{:S(2)}, u32[]{:S(2)}) collective-permute-start(f32[256,2048]{1,0:T(8,128)} %slice_bitcast_fusion.16), channel_id=1, source_target_pairs={{0,1},{1,0},{2,3},{3,2},{4,5},{5,4},{6,7},{7,6},{8,9},{9,8},{10,11... | collective-permute-start | bytes 6291464 | tf_op jit(solution)/shard_map/ppermute | solution.py:41
  476.6 44.6 %collective-permute-start.31 = (f32[256,2048]{1,0:T(8,128)}, f32[256,2048]{1,0:T(8,128)}, u32[]{:S(2)}, u32[]{:S(2)}) collective-permute-start(f32[256,2048]{1,0:T(8,128)} %slice_bitcast_fusion.18), channel_id=1, source_target_pairs={{0,1},{1,0},{2,3},{3,2},{4,5},{5,4},{6,7},{7,6},{8,9},{9,8},{10,11... | collective-permute-start | bytes 6291464 | tf_op jit(solution)/shard_map/ppermute | solution.py:41
  492.6 154.4 %collective-permute-start.38 = (f32[256,2048]{1,0:T(8,128)}, f32[256,2048]{1,0:T(8,128)}, u32[]{:S(2)}, u32[]{:S(2)}) collective-permute-start(f32[256,2048]{1,0:T(8,128)} %slice_bitcast_fusion.14), channel_id=1, source_target_pairs={{0,1},{1,0},{2,3},{3,2},{4,5},{5,4},{6,7},{7,6},{8,9},{9,8},{10,11... | collective-permute-start | bytes 6291464 | tf_op jit(solution)/shard_map/ppermute | solution.py:41
  510.7 24.0 %collective-permute-start.30 = (f32[256,1024]{1,0:T(8,128)S(1)}, f32[256,1024]{1,0:T(8,128)S(1)}, u32[]{:S(2)}, u32[]{:S(2)}) collective-permute-start(f32[256,1024]{1,0:T(8,128)S(1)} %slice.487), channel_id=1, source_target_pairs={{6,0},{7,1},{0,2},{1,3},{2,4},{3,5},{4,6},{5,7},{14,8},{15,9},{8,1... | collective-permute-start | bytes 3145736 | tf_op jit(solution)/shard_map/ppermute | solution.py:38
  512.6 33.4 %collective-permute-start.42 = (bf16[2,4,256,128]{2,3,1,0:T(8,128)(2,1)S(1)}, bf16[2,4,256,128]{2,3,1,0:T(8,128)(2,1)S(1)}, u32[]{:S(2)}, u32[]{:S(2)}) collective-permute-start(bf16[2,4,256,128]{2,3,1,0:T(8,128)(2,1)S(1)} %get-tuple-element.31), channel_id=1, source_target_pairs={{6,0},{7,1},{0,2},{1,3},{2,4},{3,5},{4,6},{5,7},{14,8},{15,9},{8,1... | collective-permute-start | bytes 1572872 | tf_op jit(solution)/shard_map/ppermute | solution.py:38
  521.3 63.4 %collective-permute-start.44 = (bf16[2,4,256,128]{2,3,1,0:T(8,128)(2,1)S(1)}, bf16[2,4,256,128]{2,3,1,0:T(8,128)(2,1)S(1)}, u32[]{:S(2)}, u32[]{:S(2)}) collective-permute-start(bf16[2,4,256,128]{2,3,1,0:T(8,128)(2,1)S(1)} %get-tuple-element.35), channel_id=1, source_target_pairs={{2,0},{3,1},{4,2},{5,3},{6,4},{7,5},{0,6},{1,7},{10,8},{11,9},{12,... | collective-permute-start | bytes 1572872 | tf_op jit(solution)/shard_map/ppermute | solution.py:38
  534.7 74.0 %collective-permute-start.45 = (bf16[2,4,256,128]{2,3,1,0:T(8,128)(2,1)S(1)}, bf16[2,4,256,128]{2,3,1,0:T(8,128)(2,1)S(1)}, u32[]{:S(2)}, u32[]{:S(2)}) collective-permute-start(bf16[2,4,256,128]{2,3,1,0:T(8,128)(2,1)S(1)} %get-tuple-element.36), channel_id=1, source_target_pairs={{4,0},{5,1},{6,2},{7,3},{0,4},{1,5},{2,6},{3,7},{12,8},{13,9},{14,... | collective-permute-start | bytes 1572872 | tf_op jit(solution)/shard_map/ppermute | solution.py:38
  545.9 36.1 %collective-permute-start.32 = (f32[256,1024]{1,0:T(8,128)S(1)}, f32[256,1024]{1,0:T(8,128)S(1)}, u32[]{:S(2)}, u32[]{:S(2)}) collective-permute-start(f32[256,1024]{1,0:T(8,128)S(1)} %slice_add_fusion.3), channel_id=1, source_target_pairs={{6,0},{7,1},{0,2},{1,3},{2,4},{3,5},{4,6},{5,7},{14,8},{15,9},{8,1... | collective-permute-start | bytes 3145736 | tf_op jit(solution)/shard_map/ppermute | solution.py:38
  546.1 63.5 %collective-permute-start.46 = (bf16[2,4,256,128]{2,3,1,0:T(8,128)(2,1)S(1)}, bf16[2,4,256,128]{2,3,1,0:T(8,128)(2,1)S(1)}, u32[]{:S(2)}, u32[]{:S(2)}) collective-permute-start(bf16[2,4,256,128]{2,3,1,0:T(8,128)(2,1)S(1)} %get-tuple-element.34), channel_id=1, source_target_pairs={{6,0},{7,1},{0,2},{1,3},{2,4},{3,5},{4,6},{5,7},{14,8},{15,9},{8,1... | collective-permute-start | bytes 1572872 | tf_op jit(solution)/shard_map/ppermute | solution.py:38
  583.3 24.3 %collective-permute-start.35 = (f32[256,1024]{1,0:T(8,128)S(1)}, f32[256,1024]{1,0:T(8,128)S(1)}, u32[]{:S(2)}, u32[]{:S(2)}) collective-permute-start(f32[256,1024]{1,0:T(8,128)S(1)} %get-tuple-element.38), channel_id=1, source_target_pairs={{2,0},{3,1},{4,2},{5,3},{6,4},{7,5},{0,6},{1,7},{10,8},{11,9},{12,... | collective-permute-start | bytes 3145736 | tf_op jit(solution)/shard_map/ppermute | solution.py:38
  608.7 23.6 %collective-permute-start.36 = (f32[256,1024]{1,0:T(8,128)}, f32[256,1024]{1,0:T(8,128)}, u32[]{:S(2)}, u32[]{:S(2)}) collective-permute-start(f32[256,1024]{1,0:T(8,128)} %slice_add_fusion.1), channel_id=1, source_target_pairs={{2,0},{3,1},{4,2},{5,3},{6,4},{7,5},{0,6},{1,7},{10,8},{11,9},{12,... | collective-permute-start | bytes 3145736 | tf_op jit(solution)/shard_map/ppermute | solution.py:38
  619.4 27.6 %collective-permute-start.34 = (f32[256,1024]{1,0:T(8,128)}, f32[256,1024]{1,0:T(8,128)}, u32[]{:S(2)}, u32[]{:S(2)}) collective-permute-start(f32[256,1024]{1,0:T(8,128)} %get-tuple-element.37), channel_id=1, source_target_pairs={{6,0},{7,1},{0,2},{1,3},{2,4},{3,5},{4,6},{5,7},{14,8},{15,9},{8,1... | collective-permute-start | bytes 3145736 | tf_op jit(solution)/shard_map/ppermute | solution.py:38
  634.6 22.8 %collective-permute-start.37 = (f32[256,1024]{1,0:T(8,128)}, f32[256,1024]{1,0:T(8,128)}, u32[]{:S(2)}, u32[]{:S(2)}) collective-permute-start(f32[256,1024]{1,0:T(8,128)} %slice_add_fusion), channel_id=1, source_target_pairs={{2,0},{3,1},{4,2},{5,3},{6,4},{7,5},{0,6},{1,7},{10,8},{11,9},{12,... | collective-permute-start | bytes 3145736 | tf_op jit(solution)/shard_map/ppermute | solution.py:38
  (71 other events, 892.6 us)
Sparse Core Ops, SparseCore 0:
  37.0 116.7 all-gather.2
  155.9 110.5 all-gather.4

commit v2 on v0

v2 whole, which is shorter than its diff:
```python
import jax
import jax.numpy as jnp
from jax import lax
from jax.experimental import pallas as pl
from jax.experimental.pallas import tpu as pltpu
from jax.sharding import PartitionSpec as P

HEAD_DIM = 128
NORM_EPS = 1e-5
ROPE_BASE = 8000000.0
UNIT = 16
SEQ = 256
HT = 128
DIM = 2048
MESH = pl.DeviceIdType.MESH
LANE = 128
SIDE = 1024
QUART = 512
PART = 32
NX = 4
LAST = 3
FAR = 6
GC = 8
GROUP = 128
UNITS = 4
INV3 = 43
OFFS = (0, 3, 7, 11)
CNTS = (3, 4, 4, 5)
ORDER = ((1, 0, 2, 3), (0, 1, 2, 3))
TWO = (0, 1)
F32 = jnp.float32
BF16 = jnp.bfloat16


def dot_nt(a, b):
    return lax.dot_general(a, b, (((1,), (1,)), ((), ())), preferred_element_type=F32)


def dot_nn(a, b):
    return lax.dot_general(a, b, (((1,), (0,)), ((), ())), preferred_element_type=F32)


def kernel(wq, wg, wu, wd, wo, hidden, gain, tab_own, out_ref, kc_ref, vc_ref,
           wbuf, stage, hbuf, tab, act, obuf, kvst, keep, psend, precv, rl, rr,
           u_recv, u_send, w_recv, w_send, w_own, w_cred, g_recv, g_send, t_recv, t_send, t_own,
           kv_recv, kv_send, kv_own, p_recv, p_send, r_recv, r_send):
    row = lax.axis_index("row")
    col = lax.axis_index("col")
    z, y = lax.div(row, NX), lax.rem(row, NX)
    x, c = lax.div(col, 2), lax.rem(col, 2)
    zs = [NX * lax.rem(z + d, NX) for d in range(NX)]
    ys = [lax.rem(y + d, NX) for d in range(NX)]
    xs = [2 * lax.rem(x + d, NX) for d in range(NX)]
    cs = [c, 1 - c]
    planes = [[a + b for b in ys] for a in zs]
    me = GC * row + col
    mine = UNIT * col + row

    def at(lin):
        return (0, lax.div(lin, GC), lax.rem(lin, GC))

    def dev_plane(dz, dy):
        return (0, planes[dz][dy], col)

    def dev_x(dx, dc):
        return (0, row, xs[dx] + cs[dc])

    plane_peers = [dev_plane(0, 1), dev_plane(0, LAST), dev_plane(1, 0), dev_plane(LAST, 0)]
    x_peers = [dev_x(o, e) for o in range(NX) for e in TWO if o + e > 0]

    kinds, goals, origins = [], [], []
    for i in range(UNITS):
        if i < 3:
            u = 3 * me + i
            kinds.append(lax.div(u, GROUP))
            v = lax.rem(u, GROUP)
            origins.append(lax.rem((mine + GROUP - i) * INV3, GROUP))
        else:
            kinds.append(3)
            v = me
            origins.append(mine)
        goals.append(GC * lax.rem(v, UNIT) + lax.div(v, UNIT))

    barrier = pltpu.get_barrier_semaphore()
    for peer in plane_peers + x_peers:
        pl.semaphore_signal(barrier, device_id=peer, device_id_type=MESH)
    arrivals = len(plane_peers) + len(x_peers)
    for lin, goal in zip(origins, goals):
        arrivals += jnp.where(goal == me, 0, 1)

        @pl.when(lin != me)
        def _():
            pl.semaphore_signal(barrier, device_id=at(lin), device_id_type=MESH)

    def unit_copies(i):
        src = wq.at[:, i] if i < 3 else wo
        dst = stage.at[:, kinds[i]]
        near = pltpu.make_async_copy(src, dst, u_recv)
        far = pltpu.make_async_remote_copy(
            src_ref=src, dst_ref=dst, send_sem=u_send.at[i], recv_sem=u_recv,
            device_id=at(goals[i]), device_id_type=MESH)
        return near, far

    def units_start():
        for i in range(UNITS):
            near, far = unit_copies(i)
            pl.when(goals[i] == me)(near.start)
            pl.when(goals[i] != me)(far.start)

    def units_wait():
        pltpu.make_async_copy(stage, stage, u_recv).wait()
        for i in range(UNITS):
            pl.when(goals[i] != me)(unit_copies(i)[1].wait_send)

    own = pl.ds(row * UNIT, UNIT)

    def own_copies(layer, k):
        if k == 0:
            pairs = [(stage.at[layer, pl.ds(0, 3)], wbuf.at[pl.ds(0, 3), own])]
        elif k == LAST:
            pairs = [(wd.at[layer], wbuf.at[pl.ds(OFFS[k], NX), own]), (stage.at[layer, LAST], wbuf.at[OFFS[k] + NX, own])]
        else:
            pairs = [((wg if k == 1 else wu).at[layer], wbuf.at[pl.ds(OFFS[k], NX), own])]
        return [pltpu.make_async_copy(a, b, w_own.at[k, i]) for i, (a, b) in enumerate(pairs)]

    def own_start(layer, k):
        for cp in own_copies(layer, k):
            cp.start()

    def own_wait(layer, k):
        for cp in own_copies(layer, k):
            cp.wait()

    own_start(0, 1)
    own_start(0, 2)
    tab_cp = pltpu.make_async_copy(tab_own, tab.at[0], t_own)
    tab_cp.start()

    def wcopy(k, half, msg, df, ds, part, tf, ts):
        slot = planes[ds][df] if half == 0 else planes[df][ds]
        lo, n = (half * SIDE, SIDE) if part is None else (half * SIDE + part * QUART, QUART)
        sl = wbuf.at[pl.ds(OFFS[k], CNTS[k]), pl.ds(slot * UNIT, UNIT), pl.ds(lo, n)]
        return pltpu.make_async_remote_copy(
            src_ref=sl, dst_ref=sl, send_sem=w_send.at[k], recv_sem=w_recv.at[k, half, msg],
            device_id=dev_plane(ts, tf) if half == 0 else dev_plane(tf, ts), device_id_type=MESH)

    def wsend(k, half, msg, df, ds, part, tf, ts):
        wcopy(k, half, msg, df, ds, part, tf, ts).start()

    def wwait(k, half, msg, df, ds, part):
        wcopy(k, half, msg, df, ds, part, 1, 0).wait_recv()

    def spread(k, half, d):
        wsend(k, half, NX * (d + 1), d, 0, None, 0, 1)
        wsend(k, half, NX * (d + 1) + 1, d, 0, None, 0, LAST)

    def e0(k):
        for half in TWO:
            wsend(k, half, 0, 0, 0, None, 1, 0)
            wsend(k, half, 1, 0, 0, None, LAST, 0)
        for half in TWO:
            spread(k, half, 0)

    def e1(k):
        for half in TWO:
            wwait(k, half, 0, LAST, 0, None)
            wwait(k, half, 1, 1, 0, None)
            wsend(k, half, 2, LAST, 0, 0, 1, 0)
            wsend(k, half, 3, 1, 0, 1, LAST, 0)
        for half in TWO:
            spread(k, half, LAST)
            spread(k, half, 1)

    def second(k, d):
        base = NX * (d + 1)
        for half in TWO:
            wwait(k, half, base, d, LAST, None)
            wwait(k, half, base + 1, d, 1, None)
            wsend(k, half, base + 2, d, LAST, 0, 0, 1)
            wsend(k, half, base + 3, d, 1, 1, 0, LAST)

    def e2(k):
        second(k, 0)

    def e3(k):
        for half in TWO:
            wwait(k, half, 2, 2, 0, 0)
            wwait(k, half, 3, 2, 0, 1)
            spread(k, half, 2)

    def e4(k):
        second(k, LAST)
        second(k, 1)

    def e5(k):
        second(k, 2)

    def e6(k):
        for half in TWO:
            for d in range(NX):
                wwait(k, half, NX * (d + 1) + 2, d, 2, 0)
                wwait(k, half, NX * (d + 1) + 3, d, 2, 1)
        total = wbuf.at[pl.ds(OFFS[k], CNTS[k]), pl.ds(0, SEQ - UNIT)]
        pltpu.make_async_remote_copy(
            src_ref=total, dst_ref=total, send_sem=w_send.at[k], recv_sem=w_recv.at[k, 0, 0],
            device_id=plane_peers[0], device_id_type=MESH).wait_send()

    def credit(k):
        for peer in plane_peers:
            pl.semaphore_signal(w_cred.at[k], device_id=peer, device_id_type=MESH)

    def begin(layer, k):
        if layer == 0:
            if k == 0:
                units_wait()
                own_start(0, 0)
                own_start(0, LAST)
        else:
            pl.semaphore_wait(w_cred.at[k], len(plane_peers))
            own_start(layer, k)
        own_wait(layer, k)
        e0(k)

    order = [(layer, k) for layer in TWO for k in ORDER[layer]]

    def stream():
        for i, (layer, k) in enumerate(order):
            yield e1(k)
            yield e2(k)
            yield begin(*order[i + 1]) if i + 1 < len(order) else None
            yield e3(k)
            yield e4(k)
            yield e5(k)
            yield e6(k)

    flow = stream()

    def w(n):
        for _ in range(n):
            next(flow)

    def gather_fns(buf, recv, send, rows, width):
        half0 = LANE * (width // LANE // 2)
        whole, lower, upper = (0, width), (0, half0), (half0, width - half0)
        sends = [
            (0, whole, FAR, 1, 0), (0, whole, 2, LAST, 0), (0, whole, 1, 0, 1),
            (FAR, lower, NX, 1, 0), (2, upper, NX, LAST, 0),
            (FAR, whole, FAR + 1, 0, 1), (2, whole, LAST, 0, 1), (NX, whole, NX + 1, 0, 1),
        ]

        def copy(msg, landed):
            slot, (lo, n), dst, dx, dc = sends[msg]
            return pltpu.make_async_remote_copy(
                src_ref=buf.at[dst if landed else slot, rows, pl.ds(lo, n)], dst_ref=buf.at[dst, rows, pl.ds(lo, n)],
                send_sem=send.at[msg], recv_sem=recv.at[msg], device_id=dev_x(dx, dc), device_id_type=MESH)

        def start(*msgs):
            for msg in msgs:
                copy(msg, False).start()

        def wait(*msgs):
            for msg in msgs:
                copy(msg, True).wait_recv()

        def f0():
            start(0, 1, 2)

        def f1():
            wait(0)
            start(3, 5)
            wait(1)
            start(4, 6)

        def f2():
            wait(2, 6)

        def f3():
            wait(3, 4)
            start(7)

        def f4():
            wait(5, 7)
            for msg in range(len(sends)):
                copy(msg, False).wait_send()

        return f0, f1, f2, f3, f4

    tok = [pl.ds(t * HT, HT) for t in TWO]
    g = [gather_fns(hbuf, g_recv.at[t], g_send.at[t], tok[t], DIM) for t in TWO]
    gt = gather_fns(tab, t_recv, t_send, pl.ds(0, SEQ), 3 * LANE)

    def norm(xf, layer):
        mean = jnp.mean(xf, axis=-1, keepdims=True)
        cen = xf - mean
        var = jnp.mean(cen * cen, axis=-1, keepdims=True)
        return (cen * lax.rsqrt(var + NORM_EPS) * gain[pl.ds(layer, 1), :]).astype(BF16)

    lane_even = lax.rem(lax.broadcasted_iota(jnp.int32, (HT, LANE), 1), 2) == 0

    def attend(t, p):
        nk = (t + 1) * HT

        def body(o, carry):
            h = hbuf[pl.ds(2 * o, 2), tok[t], :].reshape(2 * HT, DIM)
            q = dot_nt(h, wbuf[0]).astype(BF16)
            k = dot_nt(h, wbuf[1]).astype(BF16)
            v = dot_nt(h, wbuf[2]).astype(BF16)
            for e in TWO:
                slot = 2 * o + e
                cos = tab[slot, tok[t], pl.ds(0, LANE)]
                sin = tab[slot, tok[t], pl.ds(LANE, LANE)]
                pos = tab[slot, tok[t], pl.ds(2 * LANE, LANE)]

                def rope(val):
                    vf = val.astype(F32)
                    sw = jnp.where(lane_even, pltpu.roll(vf, LANE - 1, 1), pltpu.roll(vf, 1, 1))
                    return (vf * cos + sw * sin).astype(BF16)

                s_idx = lax.broadcasted_iota(jnp.int32, (HT, nk), 0) + t * HT
                t_idx = lax.broadcasted_iota(jnp.int32, (HT, nk), 1)
                first = s_idx.astype(F32) - (pos if t == 0 else jnp.concatenate([pos, pos], axis=1))
                ok = (t_idx <= s_idx) & (t_idx.astype(F32) >= first)
                for hd in TWO:
                    rs, cols = slice(e * HT, (e + 1) * HT), slice(hd * LANE, (hd + 1) * LANE)
                    kvst[slot, 0, hd, tok[t], :] = rope(k[rs, cols])
                    kvst[slot, 1, hd, tok[t], :] = v[rs, cols]
                    keys = kvst[slot, 0, hd, pl.ds(0, nk), :]
                    vals = kvst[slot, 1, hd, pl.ds(0, nk), :]
                    sc = dot_nt(rope(q[rs, cols]), keys) * (HEAD_DIM ** -0.5)
                    sc = jnp.where(ok, sc, -1e30)
                    ex = jnp.exp(sc - jnp.max(sc, axis=-1, keepdims=True))
                    pr = (ex / jnp.sum(ex, axis=-1, keepdims=True)).astype(BF16)
                    obuf[slot, tok[t], cols] = dot_nn(pr, vals).astype(BF16)
            return carry

        lax.fori_loop(2 * p, 2 * p + 2, body, 0)

    def mlp_in(t, p):
        slots = pl.ds(NX * p, NX)

        def body(j, carry):
            h = hbuf[slots, tok[t], :].reshape(NX * HT, DIM)
            gate = dot_nt(h, wbuf[OFFS[1] + j])
            up = dot_nt(h, wbuf[OFFS[2] + j])
            val = (gate * (1.0 / (1.0 + jnp.exp(-gate))) * up).astype(BF16)
            act[slots, tok[t], pl.ds(pl.multiple_of(j * SEQ, SEQ), SEQ)] = val.reshape(NX, HT, SEQ)
            return carry

        lax.fori_loop(0, NX, body, 0)

    sides = [pl.ds(side * SIDE, SIDE) for side in TWO]
    lead = (LAST, 1)

    def pcopy(t, side, o):
        return pltpu.make_async_remote_copy(
            src_ref=psend.at[o, :, sides[side]], dst_ref=precv.at[t, o, :, sides[side]], send_sem=p_send.at[side, o],
            recv_sem=p_recv.at[t, side, o], device_id=dev_x(0, 1), device_id_type=MESH)

    def mlp_out(t, side):
        def tile(n, carry):
            cols = pl.ds(pl.multiple_of(side * SIDE + n * SEQ, SEQ), SEQ)
            a = act[:, tok[t], :].reshape(GC * HT, SIDE)
            ov = obuf[:, tok[t], :].reshape(GC * HT, SEQ)
            wt = wbuf[pl.ds(OFFS[LAST], NX + 1), :, cols].reshape((NX + 1) * SEQ, SEQ)
            p = dot_nn(jnp.concatenate([a, ov], axis=1), wt).reshape(NX, 2, HT, SEQ)
            keep[t, :, :, cols] = p[:, 0]
            psend[:, :, cols] = p[:, 1]
            return carry

        lax.fori_loop(0, NX, tile, 0)
        for i in range(NX):
            pcopy(t, side, (lead[side], 2, 4 - lead[side], 0)[i]).start()

    def mlp_sent(t):
        for side in TWO:
            for o in range(NX):
                pcopy(t, side, o).wait_send()

    def rcopy(t, side, step, src):
        buf = rl if side == 0 else rr
        return pltpu.make_async_remote_copy(
            src_ref=src, dst_ref=buf.at[t, step], send_sem=r_send.at[side, t, step],
            recv_sem=r_recv.at[side, t, step], device_id=dev_x(lead[1 - side], 0), device_id_type=MESH)

    def ring0(t, side):
        o = lead[side]
        pcopy(t, side, o).wait_recv()
        keep[t, o, :, sides[side]] += precv[t, o, :, sides[side]]
        rcopy(t, side, 0, keep.at[t, o, :, sides[side]]).start()

    def ring(t, step):
        for side in TWO:
            buf = rl if side == 0 else rr
            o = 2 if step == 1 else lead[1 - side]
            pcopy(t, side, o).wait_recv()
            rcopy(t, side, step - 1, buf.at[t, step - 1]).wait_recv()
            buf[t, step - 1] += keep[t, o, :, sides[side]] + precv[t, o, :, sides[side]]
            rcopy(t, side, step, buf.at[t, step - 1]).start()

    def finish(t, layer):
        for side in TWO:
            pcopy(t, side, 0).wait_recv()
        for side in TWO:
            rcopy(t, side, 2, (rl if side == 0 else rr).at[t, 2]).wait_recv()

        def part(i, carry):
            rows = pl.ds(pl.multiple_of(i * PART, PART), PART)
            trows = pl.ds(pl.multiple_of(t * HT + i * PART, PART), PART)
            total = jnp.concatenate([rl[t, 2, rows], rr[t, 2, rows]], axis=1)
            total = total + (keep[t, 0, rows] + precv[t, 0, rows])
            xn = (out_ref[trows, :].astype(F32) + total).astype(BF16)
            out_ref[trows, :] = xn
            if layer == 0:
                hbuf[0, trows, :] = norm(xn.astype(F32), 1)
            return carry

        lax.fori_loop(0, HT // PART, part, 0)
        if layer == 0:
            g[t][0]()
        for side in TWO:
            for step in range(3):
                rcopy(t, side, step, rl.at[t, step]).wait_send()

    def kv_copies(layer, toks):
        return [
            pltpu.make_async_remote_copy(
                src_ref=kvst.at[2 * o + e, i, :, toks], dst_ref=ref.at[layer, pl.ds(2 * col, 2), toks], send_sem=kv_send,
                recv_sem=kv_recv.at[layer, i], device_id=dev_x(o, e), device_id_type=MESH)
            for o in range(NX) for e in TWO if o + e > 0 for i, ref in enumerate((kc_ref, vc_ref))
        ]

    def kv_local(layer):
        return [pltpu.make_async_copy(kvst.at[0, i], ref.at[layer, pl.ds(2 * col, 2)], kv_own.at[i]) for i, ref in enumerate((kc_ref, vc_ref))]

    def kv_start(layer, toks):
        for cp in kv_copies(layer, toks):
            cp.start()

    def kv_sent(layer):
        for cp in kv_local(layer):
            cp.start()
        total = kvst.at[pl.ds(1, GC - 1)]
        pltpu.make_async_remote_copy(src_ref=total, dst_ref=total, send_sem=kv_send, recv_sem=kv_recv.at[layer, 0],
                                     device_id=dev_x(0, 1), device_id_type=MESH).wait_send()
        for cp in kv_local(layer):
            cp.wait()

    x_cp = pltpu.make_async_copy(hidden, out_ref, t_own)
    tab_cp.wait()
    x_cp.start()
    x_cp.wait()

    def first_norm(i, carry):
        rows = pl.ds(pl.multiple_of(i * PART, PART), PART)
        hbuf[0, rows, :] = norm(out_ref[rows, :].astype(F32), 0)
        return carry

    lax.fori_loop(0, SEQ // PART, first_norm, 0)
    pl.semaphore_wait(barrier, arrivals)
    begin(0, 1)
    units_start()
    g[0][0]()
    g[1][0]()
    w(4)
    g[0][1]()
    w(2)
    g[1][1]()
    w(1)
    gt[0]()
    w(3)
    for fns in g:
        w(1)
        for fn in fns[2:]:
            fn()
    w(2)
    gt[1]()
    w(3)
    for fn in gt[2:]:
        fn()
    for t in TWO:
        for p in TWO:
            attend(t, p)
            w(1)
    credit(0)
    kv_start(0, pl.ds(0, SEQ))
    w(3)
    for t in TWO:
        for p in TWO:
            mlp_in(t, p)
            w(1)
    credit(1)
    credit(2)
    for t in TWO:
        for side in TWO:
            mlp_out(t, side)
            ring0(t, side)
            w(1)
        mlp_sent(t)
    credit(LAST)
    for (t, step), n in zip(((0, 1), (1, 1), (0, 2), (1, 2)), (1, 6, 3, 4)):
        w(n)
        ring(t, step)
    w(5)
    finish(0, 0)
    w(2)
    finish(1, 0)
    kv_sent(0)
    g[0][1]()
    g[0][2]()
    attend(0, 0)
    w(1)
    mlp_in(0, 0)
    w(1)
    g[1][1]()
    g[0][3]()
    w(1)
    g[0][4]()
    attend(0, 1)
    kv_start(1, tok[0])
    mlp_in(0, 1)
    for side in TWO:
        mlp_out(0, side)
        ring0(0, side)
    for fn in g[1][2:]:
        fn()
    attend(1, 0)
    ring(0, 1)
    attend(1, 1)
    mlp_in(1, 0)
    ring(0, 2)
    mlp_in(1, 1)
    mlp_sent(0)
    for side in TWO:
        mlp_out(1, side)
        ring0(1, side)
    finish(0, 1)
    ring(1, 1)
    ring(1, 2)
    kv_start(1, tok[1])
    finish(1, 1)
    mlp_sent(1)
    kv_sent(1)
    for layer in TWO:
        for i, ref in enumerate((kc_ref, vc_ref)):
            got = ref.at[layer, pl.ds(0, 2 * GC - 2)]
            pltpu.make_async_remote_copy(src_ref=got, dst_ref=got, send_sem=kv_send, recv_sem=kv_recv.at[layer, i],
                                         device_id=dev_x(0, 1), device_id_type=MESH).wait_recv()


def solution(mesh):
    tok_spec = P(("dp", "row", "col"))
    both = ("row", "col")
    col_spec = P(None, None, both)
    row_spec = P(None, both, None)

    def device_fn(hidden, positions, segments, ln_weight, w_qkv, w_out, w_gate, w_up, w_down):
        layers = w_qkv.shape[0]
        wq = w_qkv.transpose(0, 2, 1).reshape(layers, 3, UNIT, DIM)
        wg = w_gate.transpose(0, 2, 1).reshape(layers, NX, UNIT, DIM)
        wu = w_up.transpose(0, 2, 1).reshape(layers, NX, UNIT, DIM)
        wd = w_down.reshape(layers, NX, UNIT, DIM)

        inv_freq = ROPE_BASE ** (-2.0 * jnp.arange(HEAD_DIM // 2, dtype=F32) / HEAD_DIM)
        pos = positions[0].astype(F32)[:, None]
        angles = pos * inv_freq
        cos, sin = jnp.cos(angles), jnp.sin(angles)
        cos2 = jnp.stack([cos, cos], axis=-1).reshape(SEQ, HEAD_DIM)
        sin2 = jnp.stack([-sin, sin], axis=-1).reshape(SEQ, HEAD_DIM)
        tab_own = jnp.concatenate([cos2, sin2, jnp.broadcast_to(pos, (SEQ, HEAD_DIM))], axis=1)

        vm = pl.BlockSpec(memory_space=pltpu.VMEM)
        hb = pl.BlockSpec(memory_space=pl.ANY)
        dma = pltpu.SemaphoreType.DMA
        cache = jax.ShapeDtypeStruct((layers, 2 * GC, SEQ, HEAD_DIM), BF16)
        x_out, kc, vc = pl.pallas_call(
            kernel,
            out_shape=(jax.ShapeDtypeStruct((SEQ, DIM), BF16), cache, cache),
            in_specs=[hb] * 6 + [vm, hb],
            out_specs=(vm, hb, hb),
            scratch_shapes=[
                pltpu.VMEM((16, SEQ, DIM), BF16),
                pltpu.VMEM((2, UNITS, UNIT, DIM), BF16),
                pltpu.VMEM((GC, SEQ, DIM), BF16),
                pltpu.VMEM((GC, SEQ, 3 * LANE), F32),
                pltpu.VMEM((GC, SEQ, SIDE), BF16),
                pltpu.VMEM((GC, SEQ, SEQ), BF16),
                pltpu.VMEM((GC, 2, 2, SEQ, HEAD_DIM), BF16),
                pltpu.VMEM((2, NX, HT, DIM), F32),
                pltpu.VMEM((NX, HT, DIM), F32),
                pltpu.VMEM((2, NX, HT, DIM), F32),
                pltpu.VMEM((2, 3, HT, SIDE), F32),
                pltpu.VMEM((2, 3, HT, SIDE), F32),
                dma, dma((UNITS,)), dma((NX, 2, 20)), dma((NX,)), dma((NX, 2)), pltpu.SemaphoreType.REGULAR((NX,)),
                dma((2, GC)), dma((2, GC)), dma((GC,)), dma((GC,)), dma,
                dma((2, 2)), dma, dma((2,)), dma((2, 2, NX)), dma((2, NX)), dma((2, 2, 3)), dma((2, 2, 3)),
            ],
            compiler_params=pltpu.CompilerParams(collective_id=0, has_side_effects=True, vmem_limit_bytes=67043328),
        )(wq, wg, wu, wd, w_out, hidden[0], ln_weight.astype(F32), tab_own)
        return x_out[None], kc[None], vc[None]

    return jax.shard_map(device_fn, mesh=mesh, in_specs=(tok_spec, tok_spec, tok_spec, P(), col_spec, row_spec, col_spec, col_spec, row_spec), out_specs=(tok_spec, tok_spec, tok_spec), check_vma=False)
```

time: 1020 us -> 370 us (0.36)
  waiting for transfers between devices: 771 us -> 0 us
  Pallas kernels: 0 us -> 359 us
  matrix products: 140 us -> 0 us
  local copies, waits for them, and re-layouts: 45.3 us -> 6.78 us
  other arithmetic: 39.7 us -> 3.11 us
  between operations: 15 us -> 0.72 us
    all_gather x10 -> x0, waiting for transfers between devices: 767 us -> none  [the longest x2 217 us: device_fn(): lax.all_gather(w_down[layer_idx], group_axes, axis=0, tiled=True)]
    pallas_call x0 -> x1, Pallas kernels: none -> 359 us  [device_fn(): pl.pallas_call(kernel, out_shape=(jax.ShapeDtypeStruct((SEQ, DIM), BF16),...]
    dot_general x12 -> x0, matrix products: 140 us -> none  [the longest x2 58.5 us: device_fn(): jnp.einsum('btf,fd->btd', activated, full_down, preferred_element_type=jn...]
    convert_element_type x6 -> x0, local copies, waits for them, and re-layouts: 24.7 us -> none  [the longest x4 21.4 us: rotary(): heads_in.astype(jnp.float32)]
    another operation x6 -> x1, other arithmetic: 15 us -> 0.02 us  [device_fn(): cos2 = jnp.stack([cos, cos], axis=-1).reshape(SEQ, HEAD_DIM)]
  transfers between devices with their start and end apart: 10 -> 0, of which waited for: 10 -> 0; matrix products, arithmetic and copies ran while one was open for 21% -> 0% of each run, Pallas kernels for 0% -> 0%
where the time goes in v2:
time: 370 us
  Pallas kernels  359 us (97%)
  local copies, waits for them, and re-layouts  6.78 us (2%)
    pallas_call x1, Pallas kernels, device_fn(): pl.pallas_call(kernel, out_shape=(jax.ShapeDtypeStruct((SEQ, DIM), BF16),...  359 us

profile of v2, /device:TPU:1, one launch (start us, length us, event | category | flops | bytes accessed | tf_op | source)
XLA Modules:
  0.0 369.9 jit_solution(7968267591280096302)
XLA Ops:
  0.6 0.7 convert_element_type.14
  1.3 1.3 convert_element_type.13.gain
  2.6 0.1 broadcast_in_dim.16
  2.7 0.3 multiply_cosine_fusion
  3.1 0.1 copy.13
  3.2 0.1 reshape.171
  3.3 0.1 copy.15
  3.4 0.1 copy.14
  3.5 0.1 reshape.172
  3.6 0.1 copy.16
  3.7 0.8 pad_maximum_fusion.tab_own
  4.5 359.2 %shard_map.103 = (bf16[256,2048]{1,0:T(8,128)(2,1)}, bf16[2,16,256,128]{3,2,1,0:T(8,128)(2,1)}, bf16[2,16,256,128]{3,2,1,0:T(8,128)(2,1)}) custom-call(bf16[2,3,16,2048]{3,2,1,0:T(8,128)(2,1)} %bitcast.26, bf16[2,4,16,2048]{3,2,1,0:T(8,128)(2,1)} %bitcast.23, bf16[2,4,16,2048]{3,2,1,0:T(8,128)(2,1)} %bitcast.24, bf16[2,4,16,2048]{3,2,1,0:T(8,128)(2,1)} %bitcast.25, ...), custom_call_target="tpu_custom_call" | custom-call | tf_op jit(solution)/shard_map/pallas_call | solution.py:575
  363.7 0.0 copy-start.1
  363.7 2.5 copy.20
  366.2 0.0 copy-done.1
  366.2 0.0 copy-start
  366.2 1.3 copy.21
  367.5 1.0 copy-done
  368.5 1.3 copy.22
  (2 shorter events, 0.0 us)
Async XLA Ops:
  363.7 2.5 copy-start.1
  366.2 2.3 copy-start

commit v3 on v2

--- a/solution.py
+++ b/solution.py
@@ -26,8 +26,9 @@
 INV3 = 43
 OFFS = (0, 3, 7, 11)
 CNTS = (3, 4, 4, 5)
-ORDER = ((1, 0, 2, 3), (0, 1, 2, 3))
+ORDER = ((1, 0, 2, 3), (1, 2, 0, 3))
 TWO = (0, 1)
+AHEAD = {0: (1,), 2: (2, 3), 7: (4, 5), 8: (6,), 10: (7,)}
 F32 = jnp.float32
 BF16 = jnp.bfloat16
 
@@ -40,8 +41,8 @@
     return lax.dot_general(a, b, (((1,), (0,)), ((), ())), preferred_element_type=F32)
 
 
-def kernel(wq, wg, wu, wd, wo, hidden, gain, tab_own, out_ref, kc_ref, vc_ref,
-           wbuf, stage, hbuf, tab, act, obuf, kvst, keep, psend, precv, rl, rr,
+def kernel(wq, wg, wu, wd, wo, hidden, gain, tab_own, out_ref, kc_ref, vc_ref, stage,
+           wbuf, hbuf, tab, act, obuf, kvst, keep, psend, precv, rl, rr,
            u_recv, u_send, w_recv, w_send, w_own, w_cred, g_recv, g_send, t_recv, t_send, t_own,
            kv_recv, kv_send, kv_own, p_recv, p_send, r_recv, r_send):
     row = lax.axis_index("row")
@@ -92,25 +93,27 @@
         def _():
             pl.semaphore_signal(barrier, device_id=at(lin), device_id_type=MESH)
 
-    def unit_copies(i):
-        src = wq.at[:, i] if i < 3 else wo
-        dst = stage.at[:, kinds[i]]
-        near = pltpu.make_async_copy(src, dst, u_recv)
-        far = pltpu.make_async_remote_copy(
-            src_ref=src, dst_ref=dst, send_sem=u_send.at[i], recv_sem=u_recv,
-            device_id=at(goals[i]), device_id_type=MESH)
-        return near, far
-
-    def units_start():
+    def unit_far(layer, i):
+        return pltpu.make_async_remote_copy(
+            src_ref=wq.at[layer, i] if i < 3 else wo.at[layer], dst_ref=stage.at[layer, kinds[i]],
+            send_sem=u_send.at[layer, i], recv_sem=u_recv.at[layer], device_id=at(goals[i]), device_id_type=MESH)
+
+    def units_start(layer):
         for i in range(UNITS):
-            near, far = unit_copies(i)
-            pl.when(goals[i] == me)(near.start)
-            pl.when(goals[i] != me)(far.start)
-
-    def units_wait():
-        pltpu.make_async_copy(stage, stage, u_recv).wait()
+            @pl.when(goals[i] == me)
+            def _():
+                pltpu.make_async_copy(wq.at[layer, i] if i < 3 else wo.at[layer], stage.at[layer, kinds[i]], u_recv.at[layer]).start()
+
+            @pl.when(goals[i] != me)
+            def _():
+                unit_far(layer, i).start()
+
+    def units_wait(layer):
+        pltpu.make_async_copy(stage.at[layer], stage.at[layer], u_recv.at[layer]).wait()
         for i in range(UNITS):
-            pl.when(goals[i] != me)(unit_copies(i)[1].wait_send)
+            @pl.when(goals[i] != me)
+            def _():
+                unit_far(layer, i).wait_send()
 
     own = pl.ds(row * UNIT, UNIT)
 
@@ -210,28 +213,31 @@
             pl.semaphore_signal(w_cred.at[k], device_id=peer, device_id_type=MESH)
 
     def begin(layer, k):
-        if layer == 0:
-            if k == 0:
-                units_wait()
-                own_start(0, 0)
-                own_start(0, LAST)
-        else:
+        if k == 0:
+            units_wait(layer)
+        if layer > 0:
             pl.semaphore_wait(w_cred.at[k], len(plane_peers))
+        if layer > 0 or k in (0, LAST):
             own_start(layer, k)
         own_wait(layer, k)
         e0(k)
 
     order = [(layer, k) for layer in TWO for k in ORDER[layer]]
 
+    def start_after(step):
+        for j in AHEAD.get(step, ()):
+            begin(*order[j])
+
     def stream():
         for i, (layer, k) in enumerate(order):
             yield e1(k)
-            yield e2(k)
-            yield begin(*order[i + 1]) if i + 1 < len(order) else None
+            e2(k)
+            yield start_after(2 * i)
             yield e3(k)
             yield e4(k)
             yield e5(k)
-            yield e6(k)
+            e6(k)
+            yield start_after(2 * i + 1)
 
     flow = stream()
 
@@ -272,18 +278,21 @@
             start(4, 6)
 
         def f2():
-            wait(2, 6)
+            wait(2)
 
         def f3():
+            wait(6)
+
+        def f4():
             wait(3, 4)
             start(7)
 
-        def f4():
+        def f5():
             wait(5, 7)
             for msg in range(len(sends)):
                 copy(msg, False).wait_send()
 
-        return f0, f1, f2, f3, f4
+        return f0, f1, f2, f3, f4, f5
 
     tok = [pl.ds(t * HT, HT) for t in TWO]
     g = [gather_fns(hbuf, g_recv.at[t], g_send.at[t], tok[t], DIM) for t in TWO]
@@ -297,7 +306,7 @@
 
     lane_even = lax.rem(lax.broadcasted_iota(jnp.int32, (HT, LANE), 1), 2) == 0
 
-    def attend(t, p):
+    def attend(t, p, lo=0, hi=2):
         nk = (t + 1) * HT
 
         def body(o, carry):
@@ -305,6 +314,8 @@
             q = dot_nt(h, wbuf[0]).astype(BF16)
             k = dot_nt(h, wbuf[1]).astype(BF16)
             v = dot_nt(h, wbuf[2]).astype(BF16)
+            old = [[kvst[2 * o + e, i, hd, tok[0], :] for i in TWO] for e in TWO for hd in TWO] if t > 0 else None
+            outs = []
             for e in TWO:
                 slot = 2 * o + e
                 cos = tab[slot, tok[t], pl.ds(0, LANE)]
@@ -322,28 +333,32 @@
                 ok = (t_idx <= s_idx) & (t_idx.astype(F32) >= first)
                 for hd in TWO:
                     rs, cols = slice(e * HT, (e + 1) * HT), slice(hd * LANE, (hd + 1) * LANE)
-                    kvst[slot, 0, hd, tok[t], :] = rope(k[rs, cols])
-                    kvst[slot, 1, hd, tok[t], :] = v[rs, cols]
-                    keys = kvst[slot, 0, hd, pl.ds(0, nk), :]
-                    vals = kvst[slot, 1, hd, pl.ds(0, nk), :]
+                    keys, vals = rope(k[rs, cols]), v[rs, cols]
+                    kvst[slot, 0, hd, tok[t], :] = keys
+                    kvst[slot, 1, hd, tok[t], :] = vals
+                    if t > 0:
+                        keys = jnp.concatenate([old[2 * e + hd][0], keys], axis=0)
+                        vals = jnp.concatenate([old[2 * e + hd][1], vals], axis=0)
                     sc = dot_nt(rope(q[rs, cols]), keys) * (HEAD_DIM ** -0.5)
                     sc = jnp.where(ok, sc, -1e30)
                     ex = jnp.exp(sc - jnp.max(sc, axis=-1, keepdims=True))
                     pr = (ex / jnp.sum(ex, axis=-1, keepdims=True)).astype(BF16)
-                    obuf[slot, tok[t], cols] = dot_nn(pr, vals).astype(BF16)
+                    outs.append((slot, cols, dot_nn(pr, vals).astype(BF16)))
+            for slot, cols, val in outs:
+                obuf[slot, tok[t], cols] = val
             return carry
 
-        lax.fori_loop(2 * p, 2 * p + 2, body, 0)
-
-    def mlp_in(t, p):
-        slots = pl.ds(NX * p, NX)
+        lax.fori_loop(2 * p + lo, 2 * p + hi, body, 0)
+
+    def mlp_in(t, p, lo=0, n=4):
+        slots = pl.ds(NX * p + lo, n)
 
         def body(j, carry):
-            h = hbuf[slots, tok[t], :].reshape(NX * HT, DIM)
+            h = hbuf[slots, tok[t], :].reshape(n * HT, DIM)
             gate = dot_nt(h, wbuf[OFFS[1] + j])
             up = dot_nt(h, wbuf[OFFS[2] + j])
             val = (gate * (1.0 / (1.0 + jnp.exp(-gate))) * up).astype(BF16)
-            act[slots, tok[t], pl.ds(pl.multiple_of(j * SEQ, SEQ), SEQ)] = val.reshape(NX, HT, SEQ)
+            act[slots, tok[t], pl.ds(pl.multiple_of(j * SEQ, SEQ), SEQ)] = val.reshape(n, HT, SEQ)
             return carry
 
         lax.fori_loop(0, NX, body, 0)
@@ -415,25 +430,25 @@
             return carry
 
         lax.fori_loop(0, HT // PART, part, 0)
-        if layer == 0:
+        if layer + t == 0:
             g[t][0]()
         for side in TWO:
             for step in range(3):
                 rcopy(t, side, step, rl.at[t, step]).wait_send()
 
-    def kv_copies(layer, toks):
+    def kv_copies(layer, toks, offs):
         return [
             pltpu.make_async_remote_copy(
                 src_ref=kvst.at[2 * o + e, i, :, toks], dst_ref=ref.at[layer, pl.ds(2 * col, 2), toks], send_sem=kv_send,
                 recv_sem=kv_recv.at[layer, i], device_id=dev_x(o, e), device_id_type=MESH)
-            for o in range(NX) for e in TWO if o + e > 0 for i, ref in enumerate((kc_ref, vc_ref))
+            for o in offs for e in TWO if o + e > 0 for i, ref in enumerate((kc_ref, vc_ref))
         ]
 
     def kv_local(layer):
         return [pltpu.make_async_copy(kvst.at[0, i], ref.at[layer, pl.ds(2 * col, 2)], kv_own.at[i]) for i, ref in enumerate((kc_ref, vc_ref))]
 
-    def kv_start(layer, toks):
-        for cp in kv_copies(layer, toks):
+    def kv_start(layer, toks, offs):
+        for cp in kv_copies(layer, toks, offs):
             cp.start()
 
     def kv_sent(layer):
@@ -455,88 +470,104 @@
         hbuf[0, rows, :] = norm(out_ref[rows, :].astype(F32), 0)
         return carry
 
+    pl.semaphore_wait(barrier, arrivals)
+    near, far = (0, 1, 3), (2,)
+    (a0, a1, a2, a3, a4, a5), (b0, b1, *b_rest) = g
+    t0, t1, *t_rest = gt
+    begin(0, 1)
+    units_start(0)
     lax.fori_loop(0, SEQ // PART, first_norm, 0)
-    pl.semaphore_wait(barrier, arrivals)
-    begin(0, 1)
-    units_start()
-    g[0][0]()
-    g[1][0]()
-    w(4)
-    g[0][1]()
+    a0()
+    b0()
+    w(3)
+    a1()
     w(2)
-    g[1][1]()
+    b1()
     w(1)
-    gt[0]()
-    w(3)
+    t0()
+    w(2)
     for fns in g:
         w(1)
         for fn in fns[2:]:
             fn()
     w(2)
-    gt[1]()
-    w(3)
-    for fn in gt[2:]:
+    t1()
+    w(2)
+    for fn in t_rest:
         fn()
     for t in TWO:
         for p in TWO:
             attend(t, p)
             w(1)
     credit(0)
-    kv_start(0, pl.ds(0, SEQ))
-    w(3)
+    kv_start(0, pl.ds(0, SEQ), range(NX))
+    w(2)
     for t in TWO:
         for p in TWO:
             mlp_in(t, p)
-            w(1)
+            if t + p < 2:
+                w(1)
     credit(1)
     credit(2)
+    w(1)
     for t in TWO:
         for side in TWO:
             mlp_out(t, side)
             ring0(t, side)
-            w(1)
+            if t + side == 0:
+                units_start(1)
+                w(1)
+            else:
+                w(1 - t)
         mlp_sent(t)
     credit(LAST)
-    for (t, step), n in zip(((0, 1), (1, 1), (0, 2), (1, 2)), (1, 6, 3, 4)):
+    for (t, step), n in zip(((0, 1), (1, 1), (0, 2), (1, 2)), (3, 3, 3, 3)):
         w(n)
         ring(t, step)
-    w(5)
+    w(3)
     finish(0, 0)
     w(2)
     finish(1, 0)
     kv_sent(0)
-    g[0][1]()
-    g[0][2]()
-    attend(0, 0)
+    a2()
+    attend(0, 0, 0, 1)
+    mlp_in(0, 0, 0, 2)
+    a1()
+    b0()
     w(1)
-    mlp_in(0, 0)
+    a3()
+    attend(0, 0, 1, 2)
+    mlp_in(0, 0, 2, 2)
     w(1)
-    g[1][1]()
-    g[0][3]()
+    a4()
+    a5()
+    attend(0, 1)
     w(1)
-    g[0][4]()
-    attend(0, 1)
-    kv_start(1, tok[0])
+    b1()
     mlp_in(0, 1)
+    w(2)
     for side in TWO:
         mlp_out(0, side)
         ring0(0, side)
-    for fn in g[1][2:]:
+    kv_start(1, tok[0], near)
+    for fn in b_rest:
         fn()
     attend(1, 0)
+    attend(1, 1)
     ring(0, 1)
-    attend(1, 1)
+    kv_start(1, tok[0], far)
     mlp_in(1, 0)
-    ring(0, 2)
     mlp_in(1, 1)
     mlp_sent(0)
     for side in TWO:
         mlp_out(1, side)
         ring0(1, side)
+    ring(0, 2)
+    ring(1, 1)
+    kv_start(1, tok[1], near)
     finish(0, 1)
-    ring(1, 1)
     ring(1, 2)
-    kv_start(1, tok[1])
+    kv_start(1, tok[1], far)
     finish(1, 1)
     mlp_sent(1)
     kv_sent(1)
@@ -570,29 +601,28 @@
 
         vm = pl.BlockSpec(memory_space=pltpu.VMEM)
         hb = pl.BlockSpec(memory_space=pl.ANY)
-        dma = pltpu.SemaphoreType.DMA
+        dma, duo = pltpu.SemaphoreType.DMA, len(TWO)
         cache = jax.ShapeDtypeStruct((layers, 2 * GC, SEQ, HEAD_DIM), BF16)
-        x_out, kc, vc = pl.pallas_call(
+        x_out, kc, vc, _ = pl.pallas_call(
             kernel,
-            out_shape=(jax.ShapeDtypeStruct((SEQ, DIM), BF16), cache, cache),
+            out_shape=(jax.ShapeDtypeStruct((SEQ, DIM), BF16), cache, cache, jax.ShapeDtypeStruct((layers, UNITS, UNIT, DIM), BF16)),
             in_specs=[hb] * 6 + [vm, hb],
-            out_specs=(vm, hb, hb),
+            out_specs=(vm, hb, hb, hb),
             scratch_shapes=[
                 pltpu.VMEM((16, SEQ, DIM), BF16),
-                pltpu.VMEM((2, UNITS, UNIT, DIM), BF16),
                 pltpu.VMEM((GC, SEQ, DIM), BF16),
                 pltpu.VMEM((GC, SEQ, 3 * LANE), F32),
                 pltpu.VMEM((GC, SEQ, SIDE), BF16),
                 pltpu.VMEM((GC, SEQ, SEQ), BF16),
-                pltpu.VMEM((GC, 2, 2, SEQ, HEAD_DIM), BF16),
-                pltpu.VMEM((2, NX, HT, DIM), F32),
+                pltpu.VMEM((GC, duo, duo, SEQ, HEAD_DIM), BF16),
+                pltpu.VMEM((duo, NX, HT, DIM), F32),
                 pltpu.VMEM((NX, HT, DIM), F32),
-                pltpu.VMEM((2, NX, HT, DIM), F32),
-                pltpu.VMEM((2, 3, HT, SIDE), F32),
-                pltpu.VMEM((2, 3, HT, SIDE), F32),
-                dma, dma((UNITS,)), dma((NX, 2, 20)), dma((NX,)), dma((NX, 2)), pltpu.SemaphoreType.REGULAR((NX,)),
-                dma((2, GC)), dma((2, GC)), dma((GC,)), dma((GC,)), dma,
-                dma((2, 2)), dma, dma((2,)), dma((2, 2, NX)), dma((2, NX)), dma((2, 2, 3)), dma((2, 2, 3)),
+                pltpu.VMEM((duo, NX, HT, DIM), F32),
+                pltpu.VMEM((duo, LAST, HT, SIDE), F32),
+                pltpu.VMEM((duo, LAST, HT, SIDE), F32),
+                dma((duo,)), dma((duo, UNITS)), dma((NX, duo, 20)), dma((NX,)), dma((NX, duo)), pltpu.SemaphoreType.REGULAR((NX,)),
+                dma((duo, GC)), dma((duo, GC)), dma((GC,)), dma((GC,)), dma,
+                dma((duo, duo)), dma, dma((duo,)), dma((duo, duo, NX)), dma((duo, NX)), dma((duo, duo, LAST)), dma((duo, duo, LAST)),
             ],
             compiler_params=pltpu.CompilerParams(collective_id=0, has_side_effects=True, vmem_limit_bytes=67043328),
         )(wq, wg, wu, wd, w_out, hidden[0], ln_weight.astype(F32), tab_own)

time: 370 us -> 381 us (1.030)
  Pallas kernels: 359 us -> 369 us
    pallas_call x1, Pallas kernels: 359 us -> 369 us  [device_fn(): pl.pallas_call(kernel, out_shape=(jax.ShapeDtypeStruct((SEQ, DIM), BF16),...]
where the time goes in v3:
time: 381 us; the launch traced here: 380 us
  Pallas kernels  369 us (97%)
  local copies, waits for them, and re-layouts  6.78 us (2%)
    pallas_call x1, Pallas kernels, device_fn(): pl.pallas_call(kernel, out_shape=(jax.ShapeDtypeStruct((SEQ, DIM), BF16),...  369 us

profile of v3, /device:TPU:1, one launch (start us, length us, event | category | flops | bytes accessed | tf_op | source)
XLA Modules:
  0.0 379.7 jit_solution(14564242343609482593)
XLA Ops:
  0.6 0.7 convert_element_type.14
  1.3 1.3 convert_element_type.13.gain
  2.6 0.1 broadcast_in_dim.16
  2.7 0.3 multiply_cosine_fusion
  3.1 0.1 copy.13
  3.2 0.1 reshape.171
  3.3 0.1 copy.15
  3.4 0.1 copy.14
  3.5 0.1 reshape.172
  3.6 0.1 copy.16
  3.7 0.8 pad_maximum_fusion.tab_own
  4.5 369.0 %shard_map.103 = (bf16[256,2048]{1,0:T(8,128)(2,1)}, bf16[2,16,256,128]{3,2,1,0:T(8,128)(2,1)}, bf16[2,16,256,128]{3,2,1,0:T(8,128)(2,1)}, bf16[2,4,16,2048]{3,2,1,0:T(8,128)(2,1)}) custom-call(bf16[2,3,16,2048]{3,2,1,0:T(8,128)(2,1)} %bitcast.26, bf16[2,4,16,2048]{3,2,1,0:T(8,128)(2,1)} %bitcast.23, bf16[2,4,16,2048]{3,2,1,0:T(8,128)(2,1)} %bitcast.24, ...), custom_call_target="tpu_custom_call" | custom-call | tf_op jit(solution)/shard_map/pallas_call | solution.py:606
  373.5 0.0 copy-start.1
  373.5 2.5 copy.20
  376.0 0.0 copy-done.1
  376.0 0.0 copy-start
  376.0 1.3 copy.21
  377.3 1.0 copy-done
  378.3 1.3 copy.22
  (2 shorter events, 0.0 us)
Async XLA Ops:
  373.5 2.5 copy-start.1
  376.0 2.3 copy-start

commit v4 on v3

--- a/solution.py
+++ b/solution.py
@@ -28,7 +28,7 @@
 CNTS = (3, 4, 4, 5)
 ORDER = ((1, 0, 2, 3), (1, 2, 0, 3))
 TWO = (0, 1)
-AHEAD = {0: (1,), 2: (2, 3), 7: (4, 5), 8: (6,), 10: (7,)}
+AHEAD = {0: (1,), 2: (2,), 4: (3,), 7: (4,), 8: (5,), 10: (6,), 12: (7,)}
 F32 = jnp.float32
 BF16 = jnp.bfloat16
 
@@ -544,27 +544,28 @@
     attend(0, 1)
     w(1)
     b1()
+    kv_start(1, tok[0], near)
     mlp_in(0, 1)
     w(2)
     for side in TWO:
         mlp_out(0, side)
         ring0(0, side)
-    kv_start(1, tok[0], near)
+    kv_start(1, tok[0], far)
     for fn in b_rest:
         fn()
     attend(1, 0)
     attend(1, 1)
     ring(0, 1)
-    kv_start(1, tok[0], far)
     mlp_in(1, 0)
     mlp_in(1, 1)
     mlp_sent(0)
-    for side in TWO:
-        mlp_out(1, side)
-        ring0(1, side)
+    kv_start(1, tok[1], near)
+    mlp_out(1, 0)
+    ring0(1, 0)
     ring(0, 2)
+    mlp_out(1, 1)
+    ring0(1, 1)
     ring(1, 1)
-    kv_start(1, tok[1], near)
     finish(0, 1)
     ring(1, 2)
     kv_start(1, tok[1], far)

time: 381 us -> 356 us (0.934)
  the two profiles are of different devices: /device:TPU:1 before, /device:TPU:34 now
where the time goes in v4:
time: 356 us
  Pallas kernels  345 us (97%)
  local copies, waits for them, and re-layouts  6.78 us (2%)
    pallas_call x1, Pallas kernels, device_fn(): pl.pallas_call(kernel, out_shape=(jax.ShapeDtypeStruct((SEQ, DIM), BF16),...  345 us

profile of v4, /device:TPU:34, one launch (start us, length us, event | category | flops | bytes accessed | tf_op | source)
XLA Modules:
  0.0 355.8 jit_solution(224038724232996471)
XLA Ops:
  0.6 0.7 convert_element_type.14
  1.3 1.3 convert_element_type.13.gain
  2.6 0.1 broadcast_in_dim.16
  2.7 0.3 multiply_cosine_fusion
  3.1 0.1 copy.13
  3.2 0.1 reshape.171
  3.3 0.1 copy.15
  3.4 0.1 copy.14
  3.5 0.1 reshape.172
  3.6 0.1 copy.16
  3.7 0.8 pad_maximum_fusion.tab_own
  4.5 345.2 %shard_map.103 = (bf16[256,2048]{1,0:T(8,128)(2,1)}, bf16[2,16,256,128]{3,2,1,0:T(8,128)(2,1)}, bf16[2,16,256,128]{3,2,1,0:T(8,128)(2,1)}, bf16[2,4,16,2048]{3,2,1,0:T(8,128)(2,1)}) custom-call(bf16[2,3,16,2048]{3,2,1,0:T(8,128)(2,1)} %bitcast.26, bf16[2,4,16,2048]{3,2,1,0:T(8,128)(2,1)} %bitcast.23, bf16[2,4,16,2048]{3,2,1,0:T(8,128)(2,1)} %bitcast.24, ...), custom_call_target="tpu_custom_call" | custom-call | tf_op jit(solution)/shard_map/pallas_call | solution.py:607
  349.7 0.0 copy-start.1
  349.7 2.5 copy.20
  352.2 0.0 copy-done.1
  352.2 0.0 copy-start
  352.2 1.3 copy.21
  353.5 1.0 copy-done
  354.5 1.3 copy.22
  (2 shorter events, 0.0 us)
Async XLA Ops:
  349.7 2.5 copy-start.1
  352.2 2.3 copy-start
